TPU v7x, 32 devices: a whole 2x2x4 slice. The times are simulated.
32 devices in a mesh: mode: 8 (over z, y), row: 4 (over x, core).
Axes of the slice: x: 2, y: 2, z: 4, core: 2. Of those that a mesh axis runs over, the one named last changes fastest.
Arguments:
- density: float32 [2, 2048, 2048], P(None, 'row', 'mode'), may hold values from -6 to 6
- auxiliary: float32 [2048, 32, 2, 128], P('row', 'mode'), may hold values from -2 to 2
- hamiltonian: bfloat16 [2048, 2048], P('row'), as said below
- coupling: int32 [2, 128], replicated, may hold values from 0 to 2047, as said below
- lead_index: int32 [32], P('mode'), may hold values from 0 to 1
- mode_level: float32 [32], P('mode'), may hold values from -2 to 2
- mode_width: float32 [32], P('mode'), may hold values from 0.05 to 3
- residue: float32 [32, 2], P('mode'), may hold values from -4 to 4
- occupation: float32 [32], P('mode'), may hold values from 0 to 1
- lead_gamma: bfloat16 [2, 128, 128], replicated, may hold values from -0.5 to 0.5
Outputs:
- density_rate: float32 [2, 2048, 2048], P(None, 'row', 'mode')
- auxiliary_rate: float32 [2048, 32, 2, 128], P('row', 'mode')
Inputs may be any that keep to these rules, and one draw needn't show every extreme that they name: `coupling`: all 256 entries are distinct orbitals. `hamiltonian`: Symmetric.
All inputs are finite; a program needn't handle non-finite values.
Results may differ from a plain program's by a relative error of at most 0.0044.
Values may be sent and summed in bfloat16 or wider, within the bound.
A program may use at most 128 MiB of HBM per device.

v0:
```python
import jax
import jax.numpy as jnp
from jax import lax
from jax.sharding import PartitionSpec as P

step_size = 0.1
highest = lax.Precision.HIGHEST


def shards(
    density,
    auxiliary,
    hamiltonian,
    coupling,
    lead_index,
    mode_level,
    mode_width,
    residue,
    occupation,
    lead_gamma,
):
    panel_rows = density.shape[1]
    columns = density.shape[2]
    lead_count = coupling.shape[0]
    coupled = coupling.shape[1]
    local_modes = auxiliary.shape[1]
    row_start = lax.axis_index("row") * panel_rows
    col_start = lax.axis_index("mode") * columns
    flat_coupling = coupling.reshape(-1)
    own_columns = lax.dynamic_slice_in_dim(hamiltonian, col_start, columns, 1)
    ham_columns = lax.all_gather(own_columns, "row", axis=0, tiled=True)
    row_select = (
        row_start + jnp.arange(panel_rows, dtype=jnp.int32)[:, None] == flat_coupling[None, :]
    ).astype(jnp.float32)
    col_select = (
        col_start + jnp.arange(columns, dtype=jnp.int32)[:, None] == flat_coupling[None, :]
    ).astype(jnp.float32)
    lead_onehot = (lead_index[:, None] == jnp.arange(lead_count, dtype=jnp.int32)[None, :]).astype(
        jnp.float32
    )
    row_select_b = row_select.astype(jnp.bfloat16)
    gamma_rows = jnp.stack(
        [
            jnp.dot(
                row_select_b[:, lead_pos * coupled : (lead_pos + 1) * coupled],
                lead_gamma[lead_pos],
                preferred_element_type=jnp.float32,
            )
            for lead_pos in range(lead_count)
        ],
        axis=1,
    )

    def rates(state_rho, state_aux):
        dens_b = state_rho.astype(jnp.bfloat16)
        aux_b = state_aux.astype(jnp.bfloat16).reshape(panel_rows, -1)
        ham_aux = jnp.dot(
            hamiltonian,
            lax.all_gather(aux_b, "row", axis=0, tiled=True),
            preferred_element_type=jnp.float32,
        )
        col_block = lax.all_gather(dens_b, "row", axis=1, tiled=True)
        ham_rho = jnp.einsum(
            "an,cnt->cat", hamiltonian, col_block, preferred_element_type=jnp.float32
        )
        row_panel = lax.all_gather(dens_b, "mode", axis=2, tiled=True).reshape(2 * panel_rows, -1)
        rho_ham = jnp.dot(row_panel, ham_columns, preferred_element_type=jnp.float32).reshape(
            2, panel_rows, columns
        )
        all_select = (
            jnp.arange(row_panel.shape[1], dtype=jnp.int32)[:, None] == flat_coupling[None, :]
        ).astype(jnp.bfloat16)
        coupled_rho = jnp.dot(row_panel, all_select, preferred_element_type=jnp.float32)
        coupled_rho = coupled_rho.astype(jnp.bfloat16).reshape(2, panel_rows, lead_count, coupled)
        sources = jnp.stack(
            [
                jnp.dot(
                    coupled_rho[:, :, lead_pos, :].reshape(2 * panel_rows, coupled),
                    lead_gamma[lead_pos],
                    preferred_element_type=jnp.float32,
                ).reshape(2, panel_rows, coupled)
                for lead_pos in range(lead_count)
            ],
            axis=2,
        )
        partial_sums = jnp.einsum(
            "akcj,kl->aclj", state_aux, lead_onehot, precision=highest
        ).reshape(panel_rows, 2 * lead_count * coupled)
        panel_sums = lax.psum(partial_sums, "mode")
        full_sums = lax.all_gather(panel_sums, "row", axis=0, tiled=True).reshape(
            -1, 2, lead_count * coupled
        )
        own_sums = lax.dynamic_slice_in_dim(full_sums, row_start, panel_rows, 0)
        cross_sums = lax.dynamic_slice_in_dim(full_sums, col_start, columns, 0)
        forward = jnp.einsum("acj,tj->cat", own_sums, col_select, precision=highest)
        backward = jnp.einsum("aj,tcj->cat", row_select, cross_sums, precision=highest)
        commutator = ham_rho - rho_ham
        rho_rate = jnp.stack(
            [commutator[1] + forward[0] + backward[0], -commutator[0] + forward[1] - backward[1]]
        )
        ham_aux = ham_aux.reshape(panel_rows, local_modes, 2, coupled)
        source_rows = sources.transpose(1, 2, 0, 3)
        driven = jnp.zeros_like(state_aux)
        for lead_pos in range(lead_count):
            weight_pos = lead_onehot[:, lead_pos][None, :, None, None]
            lead_term = source_rows[:, lead_pos][:, None, :, :]
            gamma_term = gamma_rows[:, lead_pos][:, None, None, :]
            driven = (
                driven
                + weight_pos * lead_term
                - weight_pos * occupation[None, :, None, None] * gamma_term
            )
        shifted = ham_aux - mode_level[None, :, None, None] * state_aux
        decay = mode_width[None, :, None]
        res_re = residue[:, 0][None, :, None]
        res_im = residue[:, 1][None, :, None]
        aux_re = (
            shifted[:, :, 1, :]
            - decay * state_aux[:, :, 0, :]
            + res_re * driven[:, :, 0, :]
            - res_im * driven[:, :, 1, :]
        )
        aux_im = (
            -shifted[:, :, 0, :]
            - decay * state_aux[:, :, 1, :]
            + res_re * driven[:, :, 1, :]
            + res_im * driven[:, :, 0, :]
        )
        return (rho_rate, jnp.stack([aux_re, aux_im], axis=2))

    first_rho, first_aux = rates(density, auxiliary)
    middle_rho = density + 0.5 * step_size * first_rho
    middle_aux = auxiliary + 0.5 * step_size * first_aux
    second_rho, second_aux = rates(middle_rho, middle_aux)
    return (first_rho + 2.0 * second_rho, first_aux + 2.0 * second_aux)


def solution(mesh):
    in_specs = (
        P(None, "row", "mode"),
        P("row", "mode", None, None),
        P("row", None),
        P(),
        P("mode"),
        P("mode"),
        P("mode"),
        P("mode", None),
        P("mode"),
        P(),
    )
    out_specs = (P(None, "row", "mode"), P("row", "mode", None, None))
    return jax.shard_map(shards, mesh=mesh, in_specs=in_specs, out_specs=out_specs, check_vma=False)
```

profile of v0, /device:TPU:0, one launch (start us, length us, event | category | flops | bytes accessed | tf_op | source)
XLA Modules:
  0.0 540.3 jit_solution(8981585179444016876)
XLA Ops:
  7.2 2.5 convert_element_type.35
  11.3 1.6 copy.28
  14.0 4.8 fusion.11
  18.8 2.4 copy.57
  23.2 25.3 %all-gather.22.cloned.1.call-done = bf16[2048,1024]{1,0:T(8,128)(2,1)} async-done(((bf16[512,1024]{1,0:T(8,128)(2,1)}), bf16[2048,1024]{1,0:T(8,128)(2,1)}) %all-gather.22.cloned.1.call-update) | async-done | bytes 4194320 | tf_op jit(solution)/shard_map/all_gather | solution.py:59
  48.6 5.8 %fusion.94 = f32[512,1024]{1,0:T(8,128)} fusion(bf16[512,2048]{1,0:T(8,128)(2,1)S(1)} %copy-done, bf16[2048,1024]{1,0:T(8,128)(2,1)} %all-gather.22.cloned.1.call-done), kind=kOutput, calls=%fused_computation.140 | convolution fusion | flops 2147483648 | bytes 8388608 | tf_op jit(solution)/shard_map/dot_general | solution.py:57
  54.4 4.0 reshape.113
  58.5 4.9 multiply_subtract_fusion.1
  63.4 60.2 %all-gather.14.cloned.1.call-done = bf16[2,512,2048]{1,2,0:T(8,128)(2,1)} async-done(((bf16[2,512,256]{1,2,0:T(8,128)(2,1)}), bf16[2,512,2048]{1,2,0:T(8,128)(2,1)}) %all-gather.14.cloned.1.call-update) | async-done | bytes 4194320 | tf_op jit(solution)/shard_map/all_gather | solution.py:66
  123.6 6.3 %copy.29 = bf16[2,512,2048]{2,1,0:T(8,128)(2,1)} copy(bf16[2,512,2048]{1,2,0:T(8,128)(2,1)} %all-gather.14.cloned.1.call-done) | data formatting | bytes 8388608 | tf_op jit(solution)/shard_map/all_gather | solution.py:66
  129.9 4.3 fusion.30
  134.2 2.2 reshape.114
  136.5 2.2 fusion.93
  144.5 2.2 add_subtract_fusion.1
  146.8 5.4 %fusion.39 = (f32[512,4,1,128]{3,2,1,0:T(1,128)S(1)}, f32[512,4,1,128]{3,2,1,0:T(1,128)S(1)}) fusion(f32[512,4,2,128]{3,2,1,0:T(2,128)S(1)} %copy-done.11, f32[512,4,2,128]{3,2,1,0:T(2,128)S(1)} %copy-done.1, f32[512,4,2,128]{3,2,1,0:T(2,128)S(1)} %add_subtract_fusion.1, f32[4]{0:T(128)S(1)} %get-tuple-element.29, f32[4]{0:T(128)S(1)} %get-tuple-element.28, ...), kind=kLoop, calls=%fused_computation.49 | loop fusion | flops 3407872 | bytes 8388656 | tf_op jit(solution)/shard_map/sub | solution.py:118
  152.2 4.0 fusion.91
  157.5 3.3 fusion.14
  160.9 2.3 copy.58
  164.6 99.6 %all-reduce.3.cloned.1.call-done = (f32[512,512]{0,1:T(8,128)}, f32[512,512]{0,1:T(8,128)}) async-done(((f32[512,512]{0,1:T(8,128)}, f32[512,512]{0,1:T(8,128)}), (f32[512,512]{0,1:T(8,128)}, f32[512,512]{0,1:T(8,128)})) %all-reduce.3.cloned.1.call-update) | async-done | bytes 2097168 | tf_op jit(solution)/shard_map/psum | solution.py:89
  264.3 2.6 reshape.117
  267.7 14.0 %all-gather.12.cloned.1.call-done = bf16[2048,256]{1,0:T(8,128)(2,1)} async-done(((bf16[512,256]{1,0:T(8,128)(2,1)}), bf16[2048,256]{1,0:T(8,128)(2,1)}) %all-gather.12.cloned.1.call-update) | async-done | bytes 1048592 | tf_op jit(solution)/shard_map/all_gather | solution.py:31
  281.7 4.8 convolution_bitcast_fusion.4
  286.4 2.6 copy.30
  289.0 2.6 copy.31
  291.6 14.1 %all-gather.10.cloned.1.call-done = bf16[2,2048,256]{1,2,0:T(8,128)(2,1)} async-done(((bf16[2,512,256]{1,2,0:T(8,128)(2,1)}), bf16[2,2048,256]{1,2,0:T(8,128)(2,1)}) %all-gather.10.cloned.1.call-update) | async-done | bytes 2097168 | tf_op jit(solution)/shard_map/all_gather | solution.py:62
  305.7 4.1 fusion.26
  309.8 31.8 %all-gather.16.cloned.1.call-done = f32[2048,512]{0,1:T(8,128)} async-done(((f32[512,512]{0,1:T(8,128)}), f32[2048,512]{0,1:T(8,128)}) %all-gather.16.cloned.1.call-update) | async-done | bytes 4194320 | tf_op jit(solution)/shard_map/all_gather | solution.py:90
  341.6 2.0 convolution_bitcast_fusion.3
  343.6 2.1 convolution_bitcast_fusion.2
  348.7 28.9 %all-gather.26.cloned.1.call-done = bf16[2048,1024]{1,0:T(8,128)(2,1)} async-done(((bf16[512,1024]{1,0:T(8,128)(2,1)}), bf16[2048,1024]{1,0:T(8,128)(2,1)}) %all-gather.26.cloned.1.call-update) | async-done | bytes 4194320 | tf_op jit(solution)/shard_map/all_gather | solution.py:59
  377.6 5.9 %fusion.95 = f32[1024,512]{1,0:T(8,128)} fusion(bf16[2048,1024]{1,0:T(8,128)(2,1)} %all-gather.26.cloned.1.call-done, bf16[512,2048]{1,0:T(8,128)(2,1)S(1)} %copy-done), kind=kOutput, calls=%fused_computation.141 | convolution fusion | flops 2147483648 | bytes 8388608 | tf_op jit(solution)/shard_map/dot_general | solution.py:57
  383.5 4.6 copy.47
  388.0 4.8 multiply_subtract_fusion
  392.9 20.8 %all-gather.24.cloned.1.call-done = f32[2048,512]{0,1:T(8,128)} async-done(((f32[512,512]{0,1:T(8,128)}), f32[2048,512]{0,1:T(8,128)}) %all-gather.24.cloned.1.call-update) | async-done | bytes 4194320 | tf_op jit(solution)/shard_map/all_gather | solution.py:90
  413.7 2.9 convolution_bitcast_fusion.1
  416.6 3.1 convolution_bitcast_fusion
  419.7 69.0 %all-gather.20.cloned.1.call-done = bf16[2,512,2048]{1,2,0:T(8,128)(2,1)} async-done(((bf16[2,512,256]{1,2,0:T(8,128)(2,1)}), bf16[2,512,2048]{1,2,0:T(8,128)(2,1)}) %all-gather.20.cloned.1.call-update) | async-done | bytes 4194320 | tf_op jit(solution)/shard_map/all_gather | solution.py:66
  488.7 6.3 %copy.48 = bf16[2,512,2048]{2,1,0:T(8,128)(2,1)} copy(bf16[2,512,2048]{1,2,0:T(8,128)(2,1)} %all-gather.20.cloned.1.call-done) | data formatting | bytes 8388608 | tf_op jit(solution)/shard_map/all_gather | solution.py:66
  495.0 4.8 fusion.29
  499.7 2.0 reshape.120
  501.7 2.1 fusion.92
  507.0 2.3 fusion.41
  509.4 1.8 all-gather.18.cloned.1.call-done
  511.2 3.3 fusion.23
  517.0 2.5 copy.53
  519.5 3.5 add_subtract_fusion
  523.0 5.6 %multiply_subtract_fusion.2 = (f32[512,4,1,128]{3,2,1,0:T(1,128)S(1)}, f32[512,4,1,128]{3,2,1,0:T(1,128)S(1)}) fusion(f32[512,4,2,128]{3,2,1,0:T(2,128)S(1)} %copy-done.3, f32[512,4,2,128]{3,2,1,0:T(2,128)S(1)} %copy-done.10, f32[512,4,2,128]{3,2,1,0:T(2,128)S(1)} %add_subtract_fusion, f32[4]{0:T(128)S(1)} %get-tuple-element.29, f32[4]{0:T(128)S(1)} %get-tuple-element.28, ...), kind=kLoop, calls=%fused_computation.58 | loop fusion | flops 3407872 | bytes 8388656 | tf_op jit(solution)/shard_map/sub | solution.py:118
  528.7 4.6 fusion
  (107 shorter events, 22.5 us)
Async XLA Ops:
  7.2 41.4 %copy-start = (bf16[512,2048]{1,0:T(8,128)(2,1)S(1)}, bf16[512,2048]{1,0:T(8,128)(2,1)}, u32[]{:S(2)}) copy-start(bf16[512,2048]{1,0:T(8,128)(2,1)} %param.12) | copy-start | bytes 6291460
  7.2 41.4 %all-gather.22.cloned.1.call-start = ((), (), s32[]{:S(2)}) async-start(), calls=%async_computation.6 | async-start | bytes 5242880 | tf_op jit(solution)/shard_map/all_gather | solution.py:59
  11.3 2.7 copy-start.24
  11.3 112.3 %all-gather.14.cloned.1.call-start = ((), (), s32[]{:S(2)}) async-start(), calls=%async_computation.2 | async-start | bytes 4718592 | tf_op jit(solution)/shard_map/all_gather | solution.py:66
  12.9 5.9 %copy-start.6 = (f32[2,512,256]{1,2,0:T(8,128)}, f32[2,512,256]{1,2,0:T(8,128)S(1)}, u32[]{:S(2)}) copy-start(f32[2,512,256]{1,2,0:T(8,128)S(1)} %copy.28) | copy-start | bytes 3145732
  13.9 250.3 %all-reduce.3.cloned.1.call-start = ((), (), s32[]{:S(2)}) async-start(), calls=%async_computation.9 | async-start | bytes 4194304 | tf_op jit(solution)/shard_map/psum | solution.py:89
  13.9 7.4 %copy-start.25 = (f32[4,2]{0,1:T(2,128)S(1)}, f32[4,2]{0,1:T(2,128)}, u32[]{:S(2)}) copy-start(f32[4,2]{0,1:T(2,128)} %param.17) | copy-start | bytes 100
  13.9 7.4 %copy-start.26 = (f32[4]{0:T(128)S(1)}, f32[4]{0:T(128)}, u32[]{:S(2)}) copy-start(f32[4]{0:T(128)} %param.18) | copy-start | bytes 52
  13.9 7.4 %copy-start.21 = (s32[2,128]{1,0:T(2,128)S(1)}, s32[2,128]{1,0:T(2,128)}, u32[]{:S(2)}) copy-start(s32[2,128]{1,0:T(2,128)} %param.13) | copy-start | bytes 3076
  14.0 7.5 %copy-start.20 = (bf16[2,128,128]{2,1,0:T(8,128)(2,1)S(1)}, bf16[2,128,128]{2,1,0:T(8,128)(2,1)}, u32[]{:S(2)}) copy-start(bf16[2,128,128]{2,1,0:T(8,128)(2,1)} %param.19) | copy-start | bytes 196612
  23.2 120.9 %copy-start.8 = (f32[512,4,128]{2,1,0:T(4,128)}, f32[512,4,128]{2,1,0:T(4,128)S(1)}, u32[]{:S(2)}) copy-start(f32[512,4,128]{2,1,0:T(4,128)S(1)} %get-tuple-element.32) | copy-start | bytes 3145732
  54.4 4.0 copy-start.22
  143.3 1.2 copy-start.9
  144.5 2.2 copy-start.1
  144.5 2.3 copy-start.11
  144.5 2.3 copy-start.23
  152.2 4.0 copy-start.4
  156.2 1.3 copy-start.2
  163.2 118.5 %all-gather.12.cloned.1.call-start = ((), (), s32[]{:S(2)}) async-start(), calls=%async_computation.1 | async-start | bytes 1310720 | tf_op jit(solution)/shard_map/all_gather | solution.py:31
  164.0 141.7 %all-gather.10.cloned.1.call-start = ((), (), s32[]{:S(2)}) async-start(), calls=%async_computation | async-start | bytes 2621440 | tf_op jit(solution)/shard_map/all_gather | solution.py:62
  164.6 177.0 %all-gather.16.cloned.1.call-start = ((), (), s32[]{:S(2)}) async-start(), calls=%async_computation.3 | async-start | bytes 5242880 | tf_op jit(solution)/shard_map/all_gather | solution.py:90
  264.2 113.4 %all-gather.26.cloned.1.call-start = ((), (), s32[]{:S(2)}) async-start(), calls=%async_computation.8 | async-start | bytes 5242880 | tf_op jit(solution)/shard_map/all_gather | solution.py:59
  266.9 146.8 %all-gather.24.cloned.1.call-start = ((), (), s32[]{:S(2)}) async-start(), calls=%async_computation.7 | async-start | bytes 5242880 | tf_op jit(solution)/shard_map/all_gather | solution.py:90
  267.6 221.0 %all-gather.20.cloned.1.call-start = ((), (), s32[]{:S(2)}) async-start(), calls=%async_computation.5 | async-start | bytes 4718592 | tf_op jit(solution)/shard_map/all_gather | solution.py:66
  341.6 4.2 copy-start.19
  345.7 1.3 copy-start.7
  346.1 0.8 copy-start.12
  346.1 1.0 copy-start.14
  348.1 163.1 %all-gather.18.cloned.1.call-start = ((), (), s32[]{:S(2)}) async-start(), calls=%async_computation.4 | async-start | bytes 2621440 | tf_op jit(solution)/shard_map/all_gather | solution.py:62
  504.3 2.7 copy-start.27
  504.4 2.7 copy-start.16
  511.2 3.3 copy-start.17
  511.2 3.3 copy-start.18
  514.5 1.0 copy-start.13
  514.5 1.2 copy-start.15
  519.5 3.5 copy-start.3
  519.5 3.5 copy-start.10
  523.0 5.6 %copy-start.5 = (f32[512,4,1,128]{3,2,1,0:T(1,128)S(1)}, f32[512,4,1,128]{3,2,1,0:T(1,128)}, u32[]{:S(2)}) copy-start(f32[512,4,1,128]{3,2,1,0:T(1,128)} %copy-done.4) | copy-start | bytes 3145732
Sparse Core Ops, SparseCore 0:
  11.4 37.1 all-gather.21
  50.8 72.7 all-gather.13
  163.3 100.8 all-reduce.2
  265.6 15.9 all-gather.11
  283.1 22.5 all-gather.9
  307.1 34.4 all-gather.15
  343.1 34.4 all-gather.25
  379.2 34.4 all-gather.23
  415.9 72.7 all-gather.19
  490.1 21.0 all-gather.17
where the time goes:
time: 545 us; the launch traced here: 540 us
  waiting for transfers between devices  367 us (67%)
  local copies, waits for them, and re-layouts  57.9 us (11%)
  matrix products  55.5 us (10%)
  other arithmetic  44.3 us (8%)
  between operations  14.8 us (3%)
    all_gather x2, waiting for transfers between devices, rates(): lax.all_gather(dens_b, 'mode', axis=2, tiled=True)  129 us
    psum x1, waiting for transfers between devices, rates(): panel_sums = lax.psum(partial_sums, 'mode')  99.6 us
    all_gather x2, waiting for transfers between devices, rates(): lax.all_gather(aux_b, 'row', axis=0, tiled=True)  54.2 us
    all_gather x2, waiting for transfers between devices, rates(): lax.all_gather(panel_sums, 'row', axis=0, tiled=True)  52.6 us
    all_gather x2, waiting for transfers between devices, rates(): col_block = lax.all_gather(dens_b, 'row', axis=1, tiled=True)  15.9 us
    all_gather x1, waiting for transfers between devices, shards(): ham_columns = lax.all_gather(own_columns, 'row', axis=0, tiled=True)  14 us
    all_gather x2, local copies, waits for them, and re-layouts, rates(): lax.all_gather(dens_b, 'mode', axis=2, tiled=True)  12.7 us
    dot_general x2, matrix products, rates(): jnp.dot(hamiltonian, lax.all_gather(aux_b, 'row', axis=0, tiled=True), pr...  11.7 us
  transfers between devices with their start and end apart: 10, of which 10 were waited for; matrix products, arithmetic and copies ran while one was open for 17% of the time, Pallas kernels for 0%

commit v1 on v0

v1 whole, which is shorter than its diff:
```python
import functools

import jax
import jax.numpy as jnp
from jax import lax
from jax.experimental import pallas as pl
from jax.experimental.pallas import tpu as pltpu
from jax.sharding import PartitionSpec as P

step_size = 0.1
highest = lax.Precision.HIGHEST
MESH = pl.DeviceIdType.MESH
ANY = pl.BlockSpec(memory_space=pl.ANY)


class Gather:
    def __init__(self, axis, size, pieces, src, dst, stage, sems):
        self.axis, self.size, self.pieces = axis, size, pieces
        self.src, self.dst = src, dst
        self.stage = stage
        self.send, self.recv, self.local = sems
        self.me = lax.axis_index(axis)
        self.hi, self.lo = self.me // 2, self.me % 2
        self.length = size // 2

    def copy(self, source, slot, piece, kind, target):
        return pltpu.make_async_remote_copy(
            src_ref=source,
            dst_ref=self.dst(slot, piece),
            send_sem=self.send.at[kind, slot, piece],
            recv_sem=self.recv.at[slot, piece],
            device_id={self.axis: target},
            device_id_type=MESH,
        )

    def up(self, slot, source, piece):
        return self.copy(source, slot, piece, 0, self.me + 2)

    def down(self, slot, source, piece):
        return self.copy(source, slot, piece, 1, self.me - 2)

    def pair(self, slot, source, piece):
        return self.copy(source, slot, piece, 2, self.me + 1 - 2 * self.lo)

    def can_up(self, allowed=True):
        return pl.when(allowed & (self.hi < self.length - 1))

    def can_down(self, allowed=True):
        return pl.when(allowed & (self.hi > 0))

    def first(self):
        for piece in range(self.pieces):
            args = (self.me, self.src(piece), piece)
            self.can_up()(lambda: self.up(*args).start())
            self.can_down()(lambda: self.down(*args).start())
            self.pair(*args).start()

    def keep_load(self):
        for piece in range(self.pieces):
            pltpu.make_async_copy(self.src(piece), self.stage.at[piece], self.local.at[piece]).start()

    def keep_store(self):
        for piece in range(self.pieces):
            pltpu.make_async_copy(self.src(piece), self.stage.at[piece], self.local.at[piece]).wait()
            pltpu.make_async_copy(self.stage.at[piece], self.dst(self.me, piece), self.local.at[piece]).start()

    def keep_end(self):
        for piece in range(self.pieces):
            pltpu.make_async_copy(self.stage.at[piece], self.dst(self.me, piece), self.local.at[piece]).wait()

    def step(self, s):
        for piece in range(self.pieces):

            @pl.when(self.hi - 1 - s >= 0)
            def _():
                slot = self.me - 2 * (1 + s)
                args = (slot, self.dst(slot, piece), piece)
                self.pair(*args).wait_recv()
                self.can_up()(lambda: self.up(*args).start())
                self.pair(*args).start()

            @pl.when(self.hi + 1 + s < self.length)
            def _():
                slot = self.me + 2 * (1 + s)
                args = (slot, self.dst(slot, piece), piece)
                self.pair(*args).wait_recv()
                self.can_down()(lambda: self.down(*args).start())
                self.pair(*args).start()

    def finish(self):
        for line in range(self.length):
            for piece in range(self.pieces):
                slot = 2 * line + 1 - self.lo
                self.pair(slot, self.dst(slot, piece), piece).wait_recv()
        for line in range(self.length):
            for piece in range(self.pieces):
                slot = 2 * line + self.lo
                args = (slot, self.src(piece), piece)
                self.can_up(line <= self.hi)(lambda: self.up(*args).wait_send())
                self.can_down(line >= self.hi)(lambda: self.down(*args).wait_send())
                self.pair(*args).wait_send()


def exchange_kernel(n_mode, src_ref, out_ref, send, recv):
    me = lax.axis_index("mode")
    copies = []
    for d in range(1, n_mode):
        target = lax.rem(me + d, n_mode)
        origin = lax.rem(me + n_mode - d, n_mode)
        out = pltpu.make_async_remote_copy(
            src_ref=src_ref.at[target],
            dst_ref=out_ref.at[d - 1],
            send_sem=send.at[d - 1],
            recv_sem=recv.at[d - 1],
            device_id={"mode": target},
            device_id_type=MESH,
        )
        out.start()
        copies.append(out)
    for out in copies:
        out.wait()


def exchange(partial):
    n_mode = partial.shape[0]
    return pl.pallas_call(
        functools.partial(exchange_kernel, n_mode),
        out_shape=jax.ShapeDtypeStruct((n_mode - 1,) + partial.shape[1:], partial.dtype),
        in_specs=[ANY],
        out_specs=ANY,
        scratch_shapes=[
            pltpu.SemaphoreType.DMA((n_mode - 1,)),
            pltpu.SemaphoreType.DMA((n_mode - 1,)),
        ],
        compiler_params=pltpu.CompilerParams(has_side_effects=True),
    )(partial)


def gather_kernel(n_mode, n_row, wide, with_ham, *refs):
    n_in = 4 if with_ham else 3
    rho, aux, chunk = refs[:3]
    ham = refs[3] if with_ham else None
    panel, cols, aux_all, sums, cross = refs[n_in : n_in + 5]
    ham_all = refs[n_in + 5] if with_ham else None
    rest = refs[n_in + 5 + (1 if with_ham else 0) :]
    rho_stage, aux_stage, ham_stage, chunk_stage = rest[:4]
    sems = rest[4:]
    rows, columns = rho.shape[1], rho.shape[2]
    half = aux.shape[1]
    chunk_rows = chunk.shape[0]

    def panel_at(slot, piece):
        if wide:
            start = pl.multiple_of(slot * columns, columns)
            return panel.at[piece, :, pl.ds(start, columns)]
        return panel.at[slot, piece]

    def cols_at(slot, piece):
        return cols.at[piece, pl.ds(pl.multiple_of(slot * rows, rows), rows), :]

    def aux_at(slot, piece):
        return aux_all.at[pl.ds(pl.multiple_of(slot * rows + piece * half, half), half), :]

    def ham_at(slot, piece):
        return ham_all.at[pl.ds(pl.multiple_of(slot * rows, rows), rows), :]

    across = Gather("mode", n_mode, 2, lambda p: rho.at[p], panel_at, rho_stage.at[0], sems[0:3])
    down = Gather("row", n_row, 2, lambda p: rho.at[p], cols_at, rho_stage.at[1], sems[3:6])
    modes = Gather("row", n_row, 2, lambda p: aux.at[p], aux_at, aux_stage, sems[6:9])
    gathers = [across, down, modes]
    if with_ham:
        gathers.insert(2, Gather("row", n_row, 1, lambda p: ham, ham_at, ham_stage, sems[9:12]))
    chunk_send, chunk_recv, cross_send, cross_recv, chunk_local = sems[12:17]

    mode_me, row_me = lax.axis_index("mode"), lax.axis_index("row")
    per = columns // chunk_rows
    for g in gathers:
        g.first()
    for d in range(1, n_mode):
        target = lax.rem(mode_me + d, n_mode)
        pltpu.make_async_remote_copy(
            src_ref=chunk,
            dst_ref=sums.at[mode_me],
            send_sem=chunk_send.at[d - 1],
            recv_sem=chunk_recv.at[d - 1],
            device_id={"mode": target},
            device_id_type=MESH,
        ).start()
    wanted_by = (row_me * n_mode + mode_me) // per
    for d in range(1, n_row):
        pltpu.make_async_remote_copy(
            src_ref=chunk,
            dst_ref=cross.at[lax.rem(mode_me, per)],
            send_sem=cross_send.at[d - 1],
            recv_sem=cross_recv.at[lax.rem(mode_me, per)],
            device_id={"mode": wanted_by, "row": lax.rem(row_me + d, n_row)},
            device_id_type=MESH,
        ).start()
    for g in gathers:
        g.keep_load()
    pltpu.make_async_copy(chunk, chunk_stage, chunk_local).start()
    for g in gathers:
        g.keep_store()
    pltpu.make_async_copy(chunk, chunk_stage, chunk_local).wait()
    pltpu.make_async_copy(chunk_stage, sums.at[mode_me], chunk_local).start()

    across.step(0)
    for g in gathers[1:]:
        if g is not modes:
            for s in range(g.length - 1):
                g.step(s)
    if n_mode // 2 > 2:
        across.step(1)
    for s in range(modes.length - 1):
        modes.step(s)
    for s in range(2, across.length - 1):
        across.step(s)

    for g in gathers:
        g.keep_end()
        g.finish()
    pltpu.make_async_copy(chunk_stage, sums.at[mode_me], chunk_local).wait()
    for d in range(1, n_mode):
        origin = lax.rem(mode_me + n_mode - d, n_mode)
        pltpu.make_async_remote_copy(
            src_ref=chunk,
            dst_ref=sums.at[origin],
            send_sem=chunk_send.at[d - 1],
            recv_sem=chunk_recv.at[d - 1],
            device_id={"mode": origin},
            device_id_type=MESH,
        ).wait()
    other_row = lax.rem(row_me + 1, n_row)

    def cross_copy(slot, d):
        return pltpu.make_async_remote_copy(
            src_ref=chunk,
            dst_ref=cross.at[slot],
            send_sem=cross_send.at[d - 1],
            recv_sem=cross_recv.at[slot],
            device_id={"row": other_row},
            device_id_type=MESH,
        )

    for d in range(1, n_row):
        cross_copy(0, d).wait_send()

    @pl.when((mode_me * columns) // rows != row_me)
    def _():
        for slot in range(per):
            cross_copy(slot, 1).wait_recv()


def gather(n_mode, n_row, rho, aux, chunk, ham):
    _, rows, columns = rho.shape
    width = aux.shape[1]
    chunk_rows = chunk.shape[0]
    wide = columns % 128 == 0
    bf = jnp.bfloat16
    with_ham = ham is not None
    aux = aux.reshape(2, rows // 2, width)
    shapes = [
        (2, rows, n_mode * columns) if wide else (n_mode, 2, rows, columns),
        (2, n_row * rows, columns),
        (n_row * rows, width),
        (n_mode,) + chunk.shape,
        (columns // chunk_rows,) + chunk.shape,
    ]
    if with_ham:
        shapes.append((n_row * rows, columns))
    dma = pltpu.SemaphoreType.DMA

    def group(size, pieces):
        return [dma((3, size, pieces)), dma((size, pieces)), dma((pieces,))]

    return pl.pallas_call(
        functools.partial(gather_kernel, n_mode, n_row, wide, with_ham),
        out_shape=[jax.ShapeDtypeStruct(s, bf) for s in shapes],
        in_specs=[ANY] * (4 if with_ham else 3),
        out_specs=[ANY] * len(shapes),
        scratch_shapes=[
            pltpu.VMEM((2, 2, rows, columns), bf),
            pltpu.VMEM(aux.shape, bf),
            pltpu.VMEM((1, rows, columns), bf),
            pltpu.VMEM(chunk.shape, bf),
        ]
        + group(n_mode, 2)
        + group(n_row, 2)
        + group(n_row, 2)
        + group(n_row, 1)
        + [
            dma((n_mode - 1,)),
            dma((n_mode - 1,)),
            dma((n_row - 1,)),
            dma((columns // chunk_rows,)),
            dma,
        ],
        compiler_params=pltpu.CompilerParams(has_side_effects=True),
    )(*((rho, aux, chunk, ham) if with_ham else (rho, aux, chunk)))


def shards(
    n_mode,
    n_row,
    density,
    auxiliary,
    hamiltonian,
    coupling,
    lead_index,
    mode_level,
    mode_width,
    residue,
    occupation,
    lead_gamma,
):
    bf, f32 = jnp.bfloat16, jnp.float32
    rows = density.shape[1]
    columns = density.shape[2]
    lead_count, coupled = coupling.shape
    local_modes = auxiliary.shape[1]
    mode_me, row_me = lax.axis_index("mode"), lax.axis_index("row")
    row_start = row_me * rows
    col_start = mode_me * columns
    chunk_rows = rows // n_mode
    flat = coupling.reshape(-1)
    pairs = lead_count * coupled
    own_columns = lax.dynamic_slice_in_dim(hamiltonian, col_start, columns, 1)
    row_select = (row_start + jnp.arange(rows, dtype=jnp.int32)[:, None] == flat[None, :]).astype(bf)
    col_select = (col_start + jnp.arange(columns, dtype=jnp.int32)[:, None] == flat[None, :]).astype(bf)
    all_select = (jnp.arange(n_mode * columns, dtype=jnp.int32)[:, None] == flat[None, :]).astype(bf)
    onehot = (lead_index[:, None] == jnp.arange(lead_count, dtype=jnp.int32)[None, :]).astype(f32)
    gamma_rows = [
        jnp.dot(
            row_select[:, l * coupled : (l + 1) * coupled], lead_gamma[l], preferred_element_type=f32
        )
        for l in range(lead_count)
    ]
    cross_row = col_start // rows
    cross_chunk = lax.rem(mode_me, rows // columns) * (columns // chunk_rows)

    def lead_partial(state_aux):
        leads = []
        for l in range(lead_count):
            total = 0.0
            for k in range(local_modes):
                total = total + onehot[k, l] * state_aux[:, k]
            leads.append(total)
        return jnp.stack(leads, axis=2).reshape(n_mode, chunk_rows, 2 * pairs)

    def reduced(state_aux):
        partial = lead_partial(state_aux)
        own = lax.dynamic_index_in_dim(partial, mode_me, 0, keepdims=False)
        others = exchange(partial.astype(bf))
        return (own + jnp.sum(others.astype(f32), axis=0)).astype(bf)

    def rates(state_rho, state_aux, ham_all):
        rho_b = state_rho.astype(bf)
        aux_b = state_aux.astype(bf).reshape(rows, -1)
        chunk = reduced(state_aux)
        out = gather(n_mode, n_row, rho_b, aux_b, chunk, own_columns if ham_all is None else None)
        panel, cols, aux_all, sums, cross = out[:5]
        if ham_all is None:
            ham_all = out[5]
        if panel.ndim == 4:
            panel = panel.transpose(1, 2, 0, 3)
        panel = panel.reshape(2 * rows, -1)
        ham_aux = jnp.dot(hamiltonian, aux_all, preferred_element_type=f32)
        ham_rho = [jnp.dot(hamiltonian, cols[c], preferred_element_type=f32) for c in range(2)]
        rho_ham = jnp.dot(panel, ham_all, preferred_element_type=f32)
        coupled_rho = jnp.dot(panel, all_select, preferred_element_type=f32).astype(bf)
        sources = [
            jnp.dot(
                coupled_rho[:, l * coupled : (l + 1) * coupled], lead_gamma[l], preferred_element_type=f32
            )
            for l in range(lead_count)
        ]
        own = lax.dynamic_slice_in_dim(sums, cross_chunk, columns // chunk_rows, 0)
        cross = jnp.where(cross_row == row_me, own, cross).reshape(columns, 2 * pairs)
        sums = sums.reshape(rows, 2 * pairs)
        contract = (((1,), (1,)), ((), ()))
        forward = [
            lax.dot_general(
                sums[:, c * pairs : (c + 1) * pairs], col_select, contract, preferred_element_type=f32
            )
            for c in range(2)
        ]
        backward = [
            lax.dot_general(
                row_select, cross[:, c * pairs : (c + 1) * pairs], contract, preferred_element_type=f32
            )
            for c in range(2)
        ]
        rho_rate = jnp.stack(
            [
                ham_rho[1] - rho_ham[rows:] + forward[0] + backward[0],
                rho_ham[:rows] - ham_rho[0] + forward[1] - backward[1],
            ]
        )
        ham_aux = ham_aux.reshape(rows, local_modes, 2, coupled)
        pieces = []
        for k in range(local_modes):
            driven = []
            grow = sum(onehot[k, l] * gamma_rows[l] for l in range(lead_count))
            for c in range(2):
                src = sum(onehot[k, l] * sources[l][c * rows : (c + 1) * rows] for l in range(lead_count))
                driven.append(src)
            driven[0] = driven[0] - occupation[k] * grow
            driven[1] = driven[1] - occupation[k] * grow
            re, im = state_aux[:, k, 0], state_aux[:, k, 1]
            shift_re = ham_aux[:, k, 0] - mode_level[k] * re
            shift_im = ham_aux[:, k, 1] - mode_level[k] * im
            w_re, w_im = residue[k, 0], residue[k, 1]
            pieces.append(shift_im - mode_width[k] * re + w_re * driven[0] - w_im * driven[1])
            pieces.append(-shift_re - mode_width[k] * im + w_re * driven[1] + w_im * driven[0])
        aux_rate = jnp.stack(pieces, axis=1).reshape(state_aux.shape)
        return rho_rate, aux_rate, ham_all

    first_rho, first_aux, ham_all = rates(density, auxiliary, None)
    middle_rho = density + 0.5 * step_size * first_rho
    middle_aux = auxiliary + 0.5 * step_size * first_aux
    second_rho, second_aux, _ = rates(middle_rho, middle_aux, ham_all)
    return (first_rho + 2.0 * second_rho, first_aux + 2.0 * second_aux)


def solution(mesh):
    in_specs = (
        P(None, "row", "mode"),
        P("row", "mode", None, None),
        P("row", None),
        P(),
        P("mode"),
        P("mode"),
        P("mode"),
        P("mode", None),
        P("mode"),
        P(),
    )
    out_specs = (P(None, "row", "mode"), P("row", "mode", None, None))
    body = functools.partial(shards, mesh.shape["mode"], mesh.shape["row"])
    return jax.shard_map(body, mesh=mesh, in_specs=in_specs, out_specs=out_specs, check_vma=False)
```

time: 545 us -> 352 us (0.65)
  waiting for transfers between devices: 367 us -> 0 us
  Pallas kernels: 0 us -> 172 us
  other arithmetic: 44.3 us -> 82.6 us
  matrix products: 55.5 us -> 29.7 us
  between operations: 14.8 us -> 1.47 us
    all_gather x9 -> x0, waiting for transfers between devices: 266 us -> none  [the longest x2 129 us: rates(): lax.all_gather(dens_b, 'mode', axis=2, tiled=True)]
    pallas_call x0 -> x4, Pallas kernels: none -> 172 us  [the longest x2 136 us: gather(): pl.pallas_call(functools.partial(gather_kernel, n_mode, n_row, wide, with...]
    psum x1 -> x0, waiting for transfers between devices: 99.6 us -> none  [rates(): panel_sums = lax.psum(partial_sums, 'mode')]
    unnamed x0 -> x13, other arithmetic: none -> 48.8 us
    unnamed x60 -> x102, local copies, waits for them, and re-layouts: 9.96 us -> 41 us
    sub x6 -> x0, other arithmetic: 26.5 us -> none  [the longest x2 11 us: rates(): shifted[:, :, 1, :] - decay * state_aux[:, :, 0, :]]
    dot_general x20 -> x24, matrix products: 55.5 us -> 29.7 us  [the longest x2 7.07 us: shards(): jnp.dot(row_select[:, l * coupled:(l + 1) * coupled], lead_gamma[l], pref...]
    reshape x9 -> x2, local copies, waits for them, and re-layouts: 24.2 us -> 4.13 us  [lead_partial(): return jnp.stack(leads, axis=2).reshape(n_mode, chunk_rows, 2 * pairs)]
  transfers between devices with their start and end apart: 10 -> 0, of which waited for: 10 -> 0; matrix products, arithmetic and copies ran while one was open for 17% -> 0% of each run, Pallas kernels for 0% -> 0%
where the time goes in v1:
time: 352 us; the launch traced here: 349 us
  Pallas kernels  172 us (49%)
  other arithmetic  82.6 us (23%)
  local copies, waits for them, and re-layouts  63.3 us (18%)
  matrix products  29.7 us (8%)
    pallas_call x2, Pallas kernels, gather(): pl.pallas_call(functools.partial(gather_kernel, n_mode, n_row, wide, with...  136 us
    unnamed x13, other arithmetic  48.8 us
    unnamed x102, local copies, waits for them, and re-layouts  41 us
    pallas_call x2, Pallas kernels, exchange(): pl.pallas_call(functools.partial(exchange_kernel, n_mode), out_shape=jax....  36.1 us
    add x2, other arithmetic, lead_partial(): total = total + onehot[k, l] * state_aux[:, k]  12.1 us
    dot_general x2, matrix products, shards(): jnp.dot(row_select[:, l * coupled:(l + 1) * coupled], lead_gamma[l], pref...  7.07 us

profile of v1, /device:TPU:0, one launch (start us, length us, event | category | flops | bytes accessed | tf_op | source)
XLA Modules:
  0.0 349.4 jit_solution(3366692200137927321)
XLA Ops:
  10.8 2.1 convert_element_type.42.refs_0_
  15.2 2.0 copy.41
  17.2 5.3 %add_bitcast_fusion.3 = (f32[512,2,1,128]{3,0,1,2:T(8,128)S(1)}, f32[512,2,1,128]{3,0,1,2:T(8,128)S(1)}) fusion(f32[512,4,2,128]{3,0,2,1:T(8,128)S(1)} %copy.41, f32[]{:T(128)} %bitcast.3, f32[]{:T(128)} %bitcast.2, f32[]{:T(128)} %bitcast.1, f32[]{:T(128)} %bitcast, f32[]{:T(128)} %bitcast.8, f32[]{:T(128)} %bitcast.7, f32[]{:T(128)} %bitcast.6, f32[]{:T(128)} %bitcast.5), kind=kLoop, calls=%fused_computation.52 | loop fusion | flops 1835008 | bytes 3145760 | tf_op jit(solution)/shard_map/add | solution.py:346
  22.5 1.8 copy.45
  24.4 2.1 reshape.397
  27.3 19.9 %shard_map.113 = bf16[7,64,512]{2,1,0:T(8,128)(2,1)} custom-call(bf16[8,64,512]{2,1,0:T(8,128)(2,1)} %convert_element_type.45.src_ref), custom_call_target="tpu_custom_call" | custom-call | tf_op jit(solution)/shard_map/pallas_call | solution.py:126
  48.9 68.1 %shard_map.114 = (bf16[2,512,2048]{2,1,0:T(8,128)(2,1)}, bf16[2,2048,256]{2,1,0:T(8,128)(2,1)}, bf16[2048,1024]{1,0:T(8,128)(2,1)}, bf16[8,64,512]{2,1,0:T(8,128...) custom-call(bf16[2,512,256]{2,1,0:T(8,128)(2,1)} %convert_element_type.42.refs_0_, ...), custom_call_target="tpu_custom_call" | custom-call | tf_op jit(solution)/shard_map/pallas_call | solution.py:276
  118.1 3.7 %fusion.2 = bf16[1024,256]{1,0:T(8,128)(2,1)S(1)} fusion(bf16[1024,2048]{1,0:T(8,128)(2,1)} %bitcast.284, s32[256]{0:T(256)S(1)} %bitcast.274), kind=kOutput, calls=%fused_computation.4 | convolution fusion | flops 1074528256 | bytes 4719616 | tf_op jit(solution)/shard_map/dot_general | solution.py:370
  127.6 2.4 fusion.115
  133.5 1.8 copy.89
  137.0 1.8 copy.87
  138.8 1.8 copy.86
  140.6 1.8 copy.85
  142.4 1.8 copy.84
  144.2 1.8 copy.83
  146.0 1.8 copy.82
  147.8 2.6 add_convert_fusion.refs_0_
  150.4 6.1 %bitcast_dynamic-update-slice_fusion.15 = (f32[512,8,128]{2,0,1:T(8,128)S(1)}, f32[512,128]{1,0:T(8,128)S(1)}, f32[512,128]{1,0:T(8,128)S(1)}, f32[512,128]{1,0:T(8,128)}, f32[512,128]{1,0:T(8,128)S(1)}) fusion(f32[512,1,1,128]{3,0,2,1:T(8,128)S(1)} %copy-done.22, f32[512,4,2,128]{3,0,2,1:T(8,128)S(1)} %copy-done.3, f32[]{:T(128)} %bitcast.30, ...), kind=kOutput, calls=%fused_computation.118 | convolution fusion | flops 18087936 | bytes 3509760 | tf_op jit(solution)/shard_map/dot_general | solution.py:333
  156.6 2.6 bitcast_dynamic-update-slice_fusion.14
  159.2 5.5 %bitcast_dynamic-update-slice_fusion.13 = (f32[512,8,128]{2,0,1:T(8,128)S(1)}, f32[512,128]{1,0:T(8,128)S(1)}, f32[512,128]{1,0:T(8,128)S(1)}, f32[512,128]{1,0:T(8,128)}) fusion(f32[512,8,128]{2,0,1:T(8,128)S(1)} %bitcast_dynamic-update-slice_fusion.14, f32[512,1,1,128]{3,0,2,1:T(8,128)S(1)} %copy-done.21, f32[512,4,2,128]{3,0,2,1:T(8,128)S(1)} %copy-done.3, ...), kind=kLoop, calls=%fused_computation.112 | loop fusion | flops 1310720 | bytes 3407900
  164.7 2.6 bitcast_dynamic-update-slice_fusion.12
  167.3 5.3 %bitcast_dynamic-update-slice_fusion.11 = (f32[512,8,128]{2,0,1:T(8,128)S(1)}, f32[512,128]{1,0:T(8,128)S(1)}, f32[512,128]{1,0:T(8,128)S(1)}, f32[512,128]{1,0:T(8,128)}) fusion(f32[512,8,128]{2,0,1:T(8,128)S(1)} %bitcast_dynamic-update-slice_fusion.12, f32[512,1,1,128]{3,0,2,1:T(8,128)S(1)} %copy-done.19, f32[512,4,2,128]{3,0,2,1:T(8,128)S(1)} %copy-done.3, ...), kind=kLoop, calls=%fused_computation.106 | loop fusion | flops 1310720 | bytes 3407900
  172.6 2.6 bitcast_dynamic-update-slice_fusion.10
  175.2 5.3 %bitcast_dynamic-update-slice_fusion.9 = (f32[512,8,128]{2,0,1:T(8,128)S(1)}, f32[512,128]{1,0:T(8,128)S(1)}, f32[512,128]{1,0:T(8,128)S(1)}, f32[512,128]{1,0:T(8,128)}) fusion(f32[512,8,128]{2,0,1:T(8,128)S(1)} %bitcast_dynamic-update-slice_fusion.10, f32[512,1,1,128]{3,0,2,1:T(8,128)S(1)} %copy-done.17, f32[512,4,2,128]{3,0,2,1:T(8,128)S(1)} %copy-done.3, ...), kind=kLoop, calls=%fused_computation.100 | loop fusion | flops 1310720 | bytes 3407900
  180.5 2.4 bitcast_dynamic-update-slice_fusion.8
  185.9 1.8 fusion.106
  190.6 6.8 %add_bitcast_fusion.1 = (f32[512,2,1,128]{3,0,1,2:T(8,128)S(1)}, f32[512,2,1,128]{3,0,1,2:T(8,128)S(1)}) fusion(f32[512,4,2,128]{3,0,2,1:T(8,128)} %get-tuple-element.41, f32[]{:T(128)} %bitcast.3, f32[]{:T(128)} %bitcast.2, f32[]{:T(128)} %bitcast.1, f32[]{:T(128)} %bitcast, f32[]{:T(128)} %bitcast.8, f32[]{:T(128)} %bitcast.7, f32[]{:T(128)} %bitcast.6, ...), kind=kLoop, calls=%fused_computation.50 | loop fusion | flops 1835008 | bytes 3145760 | tf_op jit(solution)/shard_map/add | solution.py:346
  199.2 2.1 reshape.402
  202.2 16.3 %shard_map.115 = bf16[7,64,512]{2,1,0:T(8,128)(2,1)} custom-call(bf16[8,64,512]{2,1,0:T(8,128)(2,1)} %convert_element_type.51.src_ref), custom_call_target="tpu_custom_call" | custom-call | tf_op jit(solution)/shard_map/pallas_call | solution.py:126
  220.2 68.1 %shard_map.116 = (bf16[2,512,2048]{2,1,0:T(8,128)(2,1)}, bf16[2,2048,256]{2,1,0:T(8,128)(2,1)}, bf16[2048,1024]{1,0:T(8,128)(2,1)}, bf16[8,64,512]{2,1,0:T(8,128)(2,1)}, bf16[4,64,512]{2,1,0:T(8,128)(2,1)}) custom-call(bf16[2,512,256]{2,1,0:T(8,128)(2,1)} %add_convert_fusion.refs_0_, bf16[2,256,1024]{2,1,0:T(8,128)(2,1)} %reshape_reshape.7.refs_1_, ...), custom_call_target="tpu_custom_call" | custom-call | tf_op jit(solution)/shard_map/pallas_call | solution.py:276
  288.3 3.9 %fusion.116 = f32[1024,256]{1,0:T(8,128)S(1)} fusion(bf16[1024,2048]{1,0:T(8,128)(2,1)} %bitcast.286, bf16[2048,256]{1,0:T(8,128)(2,1)} %get-tuple-element.15), kind=kOutput, calls=%fused_computation.200 | convolution fusion | flops 1073741824 | bytes 6291456 | tf_op jit(solution)/shard_map/dot_general | solution.py:369
  298.1 2.4 fusion.117
  304.2 1.8 copy.97
  306.0 1.8 copy.96
  307.8 1.8 copy.95
  311.4 1.8 copy.93
  313.2 1.8 copy.92
  315.0 1.8 copy.91
  316.8 1.8 copy.90
  318.6 5.2 %bitcast_dynamic-update-slice_fusion.7 = (f32[512,8,128]{2,0,1:T(8,128)S(1)}, f32[512,128]{1,0:T(8,128)S(1)}, f32[512,128]{1,0:T(8,128)S(1)}) fusion(f32[512,1,1,128]{3,0,2,1:T(8,128)} %copy.90, f32[512,4,2,128]{3,0,2,1:T(8,128)} %get-tuple-element.41, f32[]{:T(128)} %bitcast.30, f32[]{:T(128)} %bitcast.26, f32[]{:T(128)} %bitcast.24, f32[]{:T(128)} %bitcast.23, ...), kind=kLoop, calls=%fused_computation.94 | loop fusion | flops 1048575 | bytes 2883608
  323.8 2.6 bitcast_dynamic-update-slice_fusion.6
  326.5 4.0 %bitcast_dynamic-update-slice_fusion.5 = (f32[512,8,128]{2,0,1:T(8,128)S(1)}, f32[512,128]{1,0:T(8,128)S(1)}, f32[512,128]{1,0:T(8,128)S(1)}) fusion(f32[512,8,128]{2,0,1:T(8,128)S(1)} %bitcast_dynamic-update-slice_fusion.6, f32[512,1,1,128]{3,0,2,1:T(8,128)S(1)} %copy-done.20, f32[512,4,2,128]{3,0,2,1:T(8,128)S(1)} %copy-done.1, f32[]{:T(128)} %bitcast.40, ...), kind=kLoop, calls=%fused_computation.88 | loop fusion | flops 1048576 | bytes 2883608
  330.5 2.6 bitcast_dynamic-update-slice_fusion.4
  333.2 3.9 %bitcast_dynamic-update-slice_fusion.3 = (f32[512,8,128]{2,0,1:T(8,128)S(1)}, f32[512,128]{1,0:T(8,128)S(1)}, f32[512,128]{1,0:T(8,128)S(1)}) fusion(f32[512,8,128]{2,0,1:T(8,128)S(1)} %bitcast_dynamic-update-slice_fusion.4, f32[512,1,1,128]{3,0,2,1:T(8,128)S(1)} %copy-done.18, f32[512,4,2,128]{3,0,2,1:T(8,128)S(1)} %copy-done.1, f32[]{:T(128)} %bitcast.49, ...), kind=kLoop, calls=%fused_computation.82 | loop fusion | flops 1048576 | bytes 2883608
  337.1 2.6 bitcast_dynamic-update-slice_fusion.2
  339.8 4.0 %bitcast_dynamic-update-slice_fusion.1 = (f32[512,8,128]{2,0,1:T(8,128)S(1)}, f32[512,128]{1,0:T(8,128)S(1)}, f32[512,128]{1,0:T(8,128)S(1)}) fusion(f32[512,8,128]{2,0,1:T(8,128)S(1)} %bitcast_dynamic-update-slice_fusion.2, f32[512,1,1,128]{3,0,2,1:T(8,128)S(1)} %copy-done.16, f32[512,4,2,128]{3,0,2,1:T(8,128)S(1)} %copy-done.1, f32[]{:T(128)} %bitcast.58, ...), kind=kLoop, calls=%fused_computation.76 | loop fusion | flops 1048576 | bytes 2883608
  343.8 2.4 bitcast_dynamic-update-slice_fusion
  346.4 2.9 copy.77
  (135 shorter events, 48.9 us)
Async XLA Ops:
  0.6 8.5 %copy-start = (bf16[512,2048]{1,0:T(8,128)(2,1)S(1)}, bf16[512,2048]{1,0:T(8,128)(2,1)}, u32[]{:S(2)}) copy-start(bf16[512,2048]{1,0:T(8,128)(2,1)} %param.12) | copy-start | bytes 6291460
  0.7 12.2 %copy-start.4 = (f32[512,4,2,128]{3,2,1,0:T(2,128)S(1)}, f32[512,4,2,128]{3,2,1,0:T(2,128)}, u32[]{:S(2)}) copy-start(f32[512,4,2,128]{3,2,1,0:T(2,128)} %param.11) | copy-start | bytes 6291460
  9.1 0.8 copy-start.32
  17.2 5.4 %copy-start.2 = (f32[512,4,2,128]{3,0,2,1:T(8,128)}, f32[512,4,2,128]{3,0,2,1:T(8,128)S(1)}, u32[]{:S(2)}) copy-start(f32[512,4,2,128]{3,0,2,1:T(8,128)S(1)} %copy.41) | copy-start | bytes 6291460
  27.3 90.7 %copy-start.34 = (s32[2,128]{1,0:T(2,128)S(1)}, s32[2,128]{1,0:T(2,128)}, u32[]{:S(2)}) copy-start(s32[2,128]{1,0:T(2,128)} %param.13) | copy-start | bytes 3076
  118.0 3.7 %copy-start.37 = (bf16[2,512,2048]{2,1,0:T(8,128)(2,1)S(1)}, bf16[2,512,2048]{2,1,0:T(8,128)(2,1)}, u32[]{:S(2)}) copy-start(bf16[2,512,2048]{2,1,0:T(8,128)(2,1)} %get-tuple-element.14) | copy-start | bytes 12582916
  118.0 3.7 %copy-start.41 = (bf16[2048,256]{1,0:T(8,128)(2,1)S(1)}, bf16[2048,256]{1,0:T(8,128)(2,1)}, u32[]{:S(2)}) copy-start(bf16[2048,256]{1,0:T(8,128)(2,1)} %get-tuple-element.15) | copy-start | bytes 3145732
  121.8 1.3 copy-start.31
  121.8 1.7 copy-start.11
  123.1 1.6 copy-start.40
  125.4 2.2 copy-start.36
  147.8 2.6 copy-start.3
  147.8 2.6 copy-start.22
  147.8 8.8 %copy-start.30 = (f32[512,1,1,128]{3,0,2,1:T(8,128)S(1)}, f32[512,1,1,128]{3,0,2,1:T(8,128)}, u32[]{:S(2)}) copy-start(f32[512,1,1,128]{3,0,2,1:T(8,128)} %copy.83) | copy-start | bytes 786436
  150.4 8.8 %copy-start.21 = (f32[512,1,1,128]{3,0,2,1:T(8,128)S(1)}, f32[512,1,1,128]{3,0,2,1:T(8,128)}, u32[]{:S(2)}) copy-start(f32[512,1,1,128]{3,0,2,1:T(8,128)} %copy.84) | copy-start | bytes 786436
  159.2 5.5 %copy-start.28 = (f32[512,1,1,128]{3,0,2,1:T(8,128)S(1)}, f32[512,1,1,128]{3,0,2,1:T(8,128)}, u32[]{:S(2)}) copy-start(f32[512,1,1,128]{3,0,2,1:T(8,128)} %copy.85) | copy-start | bytes 786436
  159.2 8.1 %copy-start.19 = (f32[512,1,1,128]{3,0,2,1:T(8,128)S(1)}, f32[512,1,1,128]{3,0,2,1:T(8,128)}, u32[]{:S(2)}) copy-start(f32[512,1,1,128]{3,0,2,1:T(8,128)} %copy.86) | copy-start | bytes 786436
  167.3 5.3 %copy-start.26 = (f32[512,1,1,128]{3,0,2,1:T(8,128)S(1)}, f32[512,1,1,128]{3,0,2,1:T(8,128)}, u32[]{:S(2)}) copy-start(f32[512,1,1,128]{3,0,2,1:T(8,128)} %copy.87) | copy-start | bytes 786436
  167.3 7.9 %copy-start.17 = (f32[512,1,1,128]{3,0,2,1:T(8,128)S(1)}, f32[512,1,1,128]{3,0,2,1:T(8,128)}, u32[]{:S(2)}) copy-start(f32[512,1,1,128]{3,0,2,1:T(8,128)} %copy.88) | copy-start | bytes 786436
  175.2 5.3 %copy-start.24 = (f32[512,1,1,128]{3,0,2,1:T(8,128)S(1)}, f32[512,1,1,128]{3,0,2,1:T(8,128)}, u32[]{:S(2)}) copy-start(f32[512,1,1,128]{3,0,2,1:T(8,128)} %copy.89) | copy-start | bytes 786436
  183.0 1.3 copy-start.6
  184.3 1.6 copy-start.5
  288.3 3.9 %copy-start.38 = (bf16[2,512,2048]{2,1,0:T(8,128)(2,1)S(1)}, bf16[2,512,2048]{2,1,0:T(8,128)(2,1)}, u32[]{:S(2)}) copy-start(bf16[2,512,2048]{2,1,0:T(8,128)(2,1)} %get-tuple-element.20) | copy-start | bytes 12582916
  292.2 1.3 copy-start.10
  292.2 1.3 copy-start.33
  293.6 1.6 copy-start.39
  295.9 2.2 copy-start.35
  300.5 1.0 copy-start.8
  300.5 1.2 copy-start.9
  304.2 14.4 %copy-start.15 = (f32[512,128]{1,0:T(8,128)S(1)}, f32[512,128]{1,0:T(8,128)}, u32[]{:S(2)}) copy-start(f32[512,128]{1,0:T(8,128)} %get-tuple-element.57) | copy-start | bytes 786436
  318.6 5.3 %copy-start.1 = (f32[512,4,2,128]{3,0,2,1:T(8,128)S(1)}, f32[512,4,2,128]{3,0,2,1:T(8,128)}, u32[]{:S(2)}) copy-start(f32[512,4,2,128]{3,0,2,1:T(8,128)} %get-tuple-element.41) | copy-start | bytes 6291460
  318.6 5.3 %copy-start.29 = (f32[512,1,1,128]{3,0,2,1:T(8,128)S(1)}, f32[512,1,1,128]{3,0,2,1:T(8,128)}, u32[]{:S(2)}) copy-start(f32[512,1,1,128]{3,0,2,1:T(8,128)} %copy.91) | copy-start | bytes 786436
  318.6 7.9 %copy-start.14 = (f32[512,128]{1,0:T(8,128)S(1)}, f32[512,128]{1,0:T(8,128)}, u32[]{:S(2)}) copy-start(f32[512,128]{1,0:T(8,128)} %get-tuple-element.53) | copy-start | bytes 786436
  318.6 7.9 %copy-start.20 = (f32[512,1,1,128]{3,0,2,1:T(8,128)S(1)}, f32[512,1,1,128]{3,0,2,1:T(8,128)}, u32[]{:S(2)}) copy-start(f32[512,1,1,128]{3,0,2,1:T(8,128)} %copy.92) | copy-start | bytes 786436
  323.8 6.7 %copy-start.27 = (f32[512,1,1,128]{3,0,2,1:T(8,128)S(1)}, f32[512,1,1,128]{3,0,2,1:T(8,128)}, u32[]{:S(2)}) copy-start(f32[512,1,1,128]{3,0,2,1:T(8,128)} %copy.93) | copy-start | bytes 786436
  326.5 6.7 %copy-start.13 = (f32[512,128]{1,0:T(8,128)S(1)}, f32[512,128]{1,0:T(8,128)}, u32[]{:S(2)}) copy-start(f32[512,128]{1,0:T(8,128)} %get-tuple-element.49) | copy-start | bytes 786436
  326.5 6.7 %copy-start.18 = (f32[512,1,1,128]{3,0,2,1:T(8,128)S(1)}, f32[512,1,1,128]{3,0,2,1:T(8,128)}, u32[]{:S(2)}) copy-start(f32[512,1,1,128]{3,0,2,1:T(8,128)} %copy.94) | copy-start | bytes 786436
  330.5 6.6 %copy-start.25 = (f32[512,1,1,128]{3,0,2,1:T(8,128)S(1)}, f32[512,1,1,128]{3,0,2,1:T(8,128)}, u32[]{:S(2)}) copy-start(f32[512,1,1,128]{3,0,2,1:T(8,128)} %copy.95) | copy-start | bytes 786436
  333.2 6.5 %copy-start.12 = (f32[512,128]{1,0:T(8,128)S(1)}, f32[512,128]{1,0:T(8,128)}, u32[]{:S(2)}) copy-start(f32[512,128]{1,0:T(8,128)} %get-tuple-element.45) | copy-start | bytes 786436
  333.2 6.5 %copy-start.16 = (f32[512,1,1,128]{3,0,2,1:T(8,128)S(1)}, f32[512,1,1,128]{3,0,2,1:T(8,128)}, u32[]{:S(2)}) copy-start(f32[512,1,1,128]{3,0,2,1:T(8,128)} %copy.96) | copy-start | bytes 786436
  337.1 6.7 %copy-start.23 = (f32[512,1,1,128]{3,0,2,1:T(8,128)S(1)}, f32[512,1,1,128]{3,0,2,1:T(8,128)}, u32[]{:S(2)}) copy-start(f32[512,1,1,128]{3,0,2,1:T(8,128)} %copy.97) | copy-start | bytes 786436
  339.8 6.5 %copy-start.7 = (f32[512,8,128]{2,0,1:T(8,128)S(1)}, f32[512,8,128]{2,0,1:T(8,128)}, u32[]{:S(2)}) copy-start(f32[512,8,128]{2,0,1:T(8,128)} %copy-done.6) | copy-start | bytes 6291460

commit v2 on v1

--- a/solution.py
+++ b/solution.py
@@ -299,6 +299,138 @@
     )(*((rho, aux, chunk, ham) if with_ham else (rho, aux, chunk)))
 
 
+def lead_partial(params, aux, local_modes, lead_count, coupled):
+    out = []
+    for c in range(2):
+        for l in range(lead_count):
+            total = params[0, 5 + l] * aux(0, c)
+            for k in range(1, local_modes):
+                total = total + params[k, 5 + l] * aux(k, c)
+            out.append(total)
+    return out
+
+
+def prepare_kernel(sizes, params, density, aux, rho_b, aux_b, partial):
+    local_modes, lead_count, coupled = sizes
+    rho_b[...] = density[...].astype(rho_b.dtype)
+    aux_b[...] = aux[...].astype(aux_b.dtype)
+
+    def piece(k, c):
+        start = (2 * k + c) * coupled
+        return aux[:, start : start + coupled]
+
+    for at, total in enumerate(lead_partial(params, piece, *sizes)):
+        partial[:, at * coupled : (at + 1) * coupled] = total.astype(partial.dtype)
+
+
+def stage_kernel(sizes, second, *refs):
+    local_modes, lead_count, coupled = sizes
+    (params, ham, aux_all, panel, ham_all, all_select, cols) = refs[:7]
+    (gamma, row_select, col_select, sums, cross, aux) = refs[7:13]
+    f32, bf = jnp.float32, jnp.bfloat16
+    pairs = lead_count * coupled
+    if second:
+        first_rho, first_aux, rho_out, aux_out = refs[13:]
+    else:
+        density, rho_out, aux_out, rho_b, aux_b, partial = refs[13:]
+
+    def dot(x, y):
+        return jnp.dot(x, y, preferred_element_type=f32)
+
+    def dot_t(x, y):
+        return lax.dot_general(x, y, (((1,), (1,)), ((), ())), preferred_element_type=f32)
+
+    h = ham[...]
+    rates = []
+    source = []
+    for c in range(2):
+        rho = panel[c]
+        part = slice(c * pairs, (c + 1) * pairs)
+        commutator = dot(h, cols[c]) - dot(rho, ham_all[...])
+        forward = dot_t(sums[:, part], col_select[...])
+        backward = dot_t(row_select[...], cross[:, part])
+        rates.append((commutator, forward, backward))
+        coupled_rho = dot(rho, all_select[...]).astype(bf)
+        source.append(
+            [dot(coupled_rho[:, l * coupled : (l + 1) * coupled], gamma[l]) for l in range(lead_count)]
+        )
+    rho_rate = (
+        rates[1][0] + rates[0][1] + rates[0][2],
+        rates[1][1] - rates[0][0] - rates[1][2],
+    )
+    for c in range(2):
+        if second:
+            rho_out[c] = first_rho[c] + 2.0 * rho_rate[c]
+        else:
+            rho_out[c] = rho_rate[c]
+            rho_b[c] = (density[c] + 0.5 * step_size * rho_rate[c]).astype(bf)
+    grow = [
+        dot(row_select[:, l * coupled : (l + 1) * coupled], gamma[l]) for l in range(lead_count)
+    ]
+    totals = [[0.0] * lead_count for _ in range(2)]
+    for k in range(local_modes):
+        cut = [slice((2 * k + c) * coupled, (2 * k + c + 1) * coupled) for c in range(2)]
+        both = slice(2 * k * coupled, 2 * (k + 1) * coupled)
+        ham_aux = dot(h, aux_all[:, both])
+        level, width, w_re, w_im, occ = [params[k, i] for i in range(5)]
+        hot = [params[k, 5 + l] for l in range(lead_count)]
+        state = []
+        for c in range(2):
+            value = aux[:, cut[c]]
+            if second:
+                value = value + 0.5 * step_size * first_aux[:, cut[c]]
+            state.append(value)
+        rows_gamma = sum(hot[l] * grow[l] for l in range(lead_count))
+        b_re, b_im = [
+            sum(hot[l] * source[c][l] for l in range(lead_count)) - occ * rows_gamma for c in range(2)
+        ]
+        shift_re = ham_aux[:, :coupled] - level * state[0]
+        shift_im = ham_aux[:, coupled:] - level * state[1]
+        rate = (
+            shift_im - width * state[0] + w_re * b_re - w_im * b_im,
+            w_re * b_im + w_im * b_re - shift_re - width * state[1],
+        )
+        for c in range(2):
+            if second:
+                aux_out[:, cut[c]] = first_aux[:, cut[c]] + 2.0 * rate[c]
+            else:
+                aux_out[:, cut[c]] = rate[c]
+                middle = state[c] + 0.5 * step_size * rate[c]
+                aux_b[:, cut[c]] = middle.astype(bf)
+                for l in range(lead_count):
+                    totals[c][l] = totals[c][l] + hot[l] * middle
+    if not second:
+        for c in range(2):
+            for l in range(lead_count):
+                start = c * pairs + l * coupled
+                partial[:, start : start + coupled] = totals[c][l].astype(bf)
+
+
+def blocked(rows, block, shape, dim):
+    if dim is None:
+        return pl.BlockSpec(shape, lambda i: (0,) * len(shape))
+    sizes = tuple(block if d == dim else size for d, size in enumerate(shape))
+    return pl.BlockSpec(sizes, lambda i: tuple(i if d == dim else 0 for d in range(len(shape))))
+
+
+def call(kernel, rows, inputs, outputs):
+    block = 128 if rows % 128 == 0 else rows
+    in_specs = [
+        pl.BlockSpec(memory_space=pltpu.SMEM) if dim == "smem" else blocked(rows, block, x.shape, dim)
+        for x, dim in inputs
+    ]
+    return pl.pallas_call(
+        kernel,
+        grid=(rows // block,),
+        out_shape=[jax.ShapeDtypeStruct(shape, dtype) for shape, dtype, _ in outputs],
+        in_specs=in_specs,
+        out_specs=[blocked(rows, block, shape, dim) for shape, _, dim in outputs],
+        compiler_params=pltpu.CompilerParams(
+            dimension_semantics=("arbitrary",), vmem_limit_bytes=56 * 2**20
+        ),
+    )(*[x for x, _ in inputs])
+
+
 def shards(
     n_mode,
     n_row,
@@ -329,97 +461,78 @@
     col_select = (col_start + jnp.arange(columns, dtype=jnp.int32)[:, None] == flat[None, :]).astype(bf)
     all_select = (jnp.arange(n_mode * columns, dtype=jnp.int32)[:, None] == flat[None, :]).astype(bf)
     onehot = (lead_index[:, None] == jnp.arange(lead_count, dtype=jnp.int32)[None, :]).astype(f32)
-    gamma_rows = [
-        jnp.dot(
-            row_select[:, l * coupled : (l + 1) * coupled], lead_gamma[l], preferred_element_type=f32
-        )
-        for l in range(lead_count)
-    ]
+    params = jnp.concatenate(
+        [mode_level[:, None], mode_width[:, None], residue, occupation[:, None], onehot], axis=1
+    )
+    aux = auxiliary.reshape(rows, -1)
+    width = aux.shape[1]
+    sizes = (local_modes, lead_count, coupled)
     cross_row = col_start // rows
     cross_chunk = lax.rem(mode_me, rows // columns) * (columns // chunk_rows)
 
-    def lead_partial(state_aux):
-        leads = []
-        for l in range(lead_count):
-            total = 0.0
-            for k in range(local_modes):
-                total = total + onehot[k, l] * state_aux[:, k]
-            leads.append(total)
-        return jnp.stack(leads, axis=2).reshape(n_mode, chunk_rows, 2 * pairs)
-
-    def reduced(state_aux):
-        partial = lead_partial(state_aux)
+    rho_shape, aux_shape, sum_shape = density.shape, aux.shape, (rows, 2 * pairs)
+
+    def moved(rho_b, aux_b, partial, ham):
+        partial = partial.reshape(n_mode, chunk_rows, 2 * pairs)
         own = lax.dynamic_index_in_dim(partial, mode_me, 0, keepdims=False)
-        others = exchange(partial.astype(bf))
-        return (own + jnp.sum(others.astype(f32), axis=0)).astype(bf)
-
-    def rates(state_rho, state_aux, ham_all):
-        rho_b = state_rho.astype(bf)
-        aux_b = state_aux.astype(bf).reshape(rows, -1)
-        chunk = reduced(state_aux)
-        out = gather(n_mode, n_row, rho_b, aux_b, chunk, own_columns if ham_all is None else None)
+        others = exchange(partial)
+        chunk = (own.astype(f32) + jnp.sum(others.astype(f32), axis=0)).astype(bf)
+        out = gather(n_mode, n_row, rho_b, aux_b, chunk, ham)
         panel, cols, aux_all, sums, cross = out[:5]
-        if ham_all is None:
-            ham_all = out[5]
         if panel.ndim == 4:
-            panel = panel.transpose(1, 2, 0, 3)
-        panel = panel.reshape(2 * rows, -1)
-        ham_aux = jnp.dot(hamiltonian, aux_all, preferred_element_type=f32)
-        ham_rho = [jnp.dot(hamiltonian, cols[c], preferred_element_type=f32) for c in range(2)]
-        rho_ham = jnp.dot(panel, ham_all, preferred_element_type=f32)
-        coupled_rho = jnp.dot(panel, all_select, preferred_element_type=f32).astype(bf)
-        sources = [
-            jnp.dot(
-                coupled_rho[:, l * coupled : (l + 1) * coupled], lead_gamma[l], preferred_element_type=f32
-            )
-            for l in range(lead_count)
-        ]
+            panel = panel.transpose(1, 2, 0, 3).reshape(2, rows, -1)
         own = lax.dynamic_slice_in_dim(sums, cross_chunk, columns // chunk_rows, 0)
         cross = jnp.where(cross_row == row_me, own, cross).reshape(columns, 2 * pairs)
-        sums = sums.reshape(rows, 2 * pairs)
-        contract = (((1,), (1,)), ((), ()))
-        forward = [
-            lax.dot_general(
-                sums[:, c * pairs : (c + 1) * pairs], col_select, contract, preferred_element_type=f32
-            )
-            for c in range(2)
-        ]
-        backward = [
-            lax.dot_general(
-                row_select, cross[:, c * pairs : (c + 1) * pairs], contract, preferred_element_type=f32
-            )
-            for c in range(2)
-        ]
-        rho_rate = jnp.stack(
-            [
-                ham_rho[1] - rho_ham[rows:] + forward[0] + backward[0],
-                rho_ham[:rows] - ham_rho[0] + forward[1] - backward[1],
-            ]
-        )
-        ham_aux = ham_aux.reshape(rows, local_modes, 2, coupled)
-        pieces = []
-        for k in range(local_modes):
-            driven = []
-            grow = sum(onehot[k, l] * gamma_rows[l] for l in range(lead_count))
-            for c in range(2):
-                src = sum(onehot[k, l] * sources[l][c * rows : (c + 1) * rows] for l in range(lead_count))
-                driven.append(src)
-            driven[0] = driven[0] - occupation[k] * grow
-            driven[1] = driven[1] - occupation[k] * grow
-            re, im = state_aux[:, k, 0], state_aux[:, k, 1]
-            shift_re = ham_aux[:, k, 0] - mode_level[k] * re
-            shift_im = ham_aux[:, k, 1] - mode_level[k] * im
-            w_re, w_im = residue[k, 0], residue[k, 1]
-            pieces.append(shift_im - mode_width[k] * re + w_re * driven[0] - w_im * driven[1])
-            pieces.append(-shift_re - mode_width[k] * im + w_re * driven[1] + w_im * driven[0])
-        aux_rate = jnp.stack(pieces, axis=1).reshape(state_aux.shape)
-        return rho_rate, aux_rate, ham_all
-
-    first_rho, first_aux, ham_all = rates(density, auxiliary, None)
-    middle_rho = density + 0.5 * step_size * first_rho
-    middle_aux = auxiliary + 0.5 * step_size * first_aux
-    second_rho, second_aux, _ = rates(middle_rho, middle_aux, ham_all)
-    return (first_rho + 2.0 * second_rho, first_aux + 2.0 * second_aux)
+        return panel, cols, aux_all, sums.reshape(rows, 2 * pairs), cross, out[5:]
+
+    def stage(second, ham_all, panel, cols, aux_all, sums, cross, extra, outputs):
+        inputs = [
+            (params, "smem"),
+            (hamiltonian, 0),
+            (aux_all, None),
+            (panel, 1),
+            (ham_all, None),
+            (all_select, None),
+            (cols, None),
+            (lead_gamma, None),
+            (row_select, 0),
+            (col_select, None),
+            (sums, 0),
+            (cross, None),
+            (aux, 0),
+        ] + extra
+        return call(functools.partial(stage_kernel, sizes, second), rows, inputs, outputs)
+
+    rho_b, aux_b, partial = call(
+        functools.partial(prepare_kernel, sizes),
+        rows,
+        [(params, "smem"), (density, 1), (aux, 0)],
+        [(rho_shape, bf, 1), (aux_shape, bf, 0), (sum_shape, bf, 0)],
+    )
+    *blocks, extra = moved(rho_b, aux_b, partial, own_columns)
+    ham_all = extra[0]
+    first_rho, first_aux, rho_b, aux_b, partial = stage(
+        False,
+        ham_all,
+        *blocks,
+        [(density, 1)],
+        [
+            (rho_shape, f32, 1),
+            (aux_shape, f32, 0),
+            (rho_shape, bf, 1),
+            (aux_shape, bf, 0),
+            (sum_shape, bf, 0),
+        ],
+    )
+    *blocks, _ = moved(rho_b, aux_b, partial, None)
+    rho_out, aux_out = stage(
+        True,
+        ham_all,
+        *blocks,
+        [(first_rho, 1), (first_aux, 0)],
+        [(rho_shape, f32, 1), (aux_shape, f32, 0)],
+    )
+    return rho_out, aux_out.reshape(auxiliary.shape)
 
 
 def solution(mesh):

time: 352 us -> 233 us (0.66)
  other arithmetic: 82.6 us -> 14.4 us
  local copies, waits for them, and re-layouts: 63.3 us -> 13.2 us
  Pallas kernels: 172 us -> 204 us
  matrix products: 29.7 us -> 0 us
    unnamed x13 -> x0, other arithmetic: 48.8 us -> none
    unnamed x102 -> x1, local copies, waits for them, and re-layouts: 41 us -> 0.76 us
    pallas_call x0 -> x3, Pallas kernels: none -> 31.9 us  [call(): pl.pallas_call(kernel, grid=(rows // block,), out_shape=[jax.ShapeDtypeSt...]
    dot_general x24 -> x0, matrix products: 29.7 us -> none  [the longest x2 7.07 us: shards(): jnp.dot(row_select[:, l * coupled:(l + 1) * coupled], lead_gamma[l], pref...]
    add x4 -> x0, other arithmetic: 13.4 us -> none  [the longest x2 12.1 us: lead_partial(): total = total + onehot[k, l] * state_aux[:, k]]
    slice x7 -> x0, local copies, waits for them, and re-layouts: 9.43 us -> none  [the longest x2 2.76 us: rates(): shift_re = ham_aux[:, k, 0] - mode_level[k] * re]
    another operation x4 -> x0, local copies, waits for them, and re-layouts: 6.91 us -> none  [the longest x2 3.59 us: lead_partial(): return jnp.stack(leads, axis=2).reshape(n_mode, chunk_rows, 2 * pairs)]
    another operation x4 -> x0, other arithmetic: 5.04 us -> none  [the longest x2 4.9 us: rates(): aux_rate = jnp.stack(pieces, axis=1).reshape(state_aux.shape)]
where the time goes in v2:
time: 233 us
  Pallas kernels  204 us (88%)
  other arithmetic  14.4 us (6%)
  local copies, waits for them, and re-layouts  13.2 us (6%)
    pallas_call x2, Pallas kernels, gather(): pl.pallas_call(functools.partial(gather_kernel, n_mode, n_row, wide, with...  136 us
    pallas_call x2, Pallas kernels, exchange(): pl.pallas_call(functools.partial(exchange_kernel, n_mode), out_shape=jax....  36.1 us
    pallas_call x3, Pallas kernels, call(): pl.pallas_call(kernel, grid=(rows // block,), out_shape=[jax.ShapeDtypeSt...  31.9 us

profile of v2, /device:TPU:0, one launch (start us, length us, event | category | flops | bytes accessed | tf_op | source)
XLA Modules:
  0.0 232.5 jit_solution(8930597191676856462)
XLA Ops:
  0.7 0.7 fusion.3
  1.4 0.7 copy.12
  2.2 0.7 copy.13
  2.9 0.8 copy.14
  3.7 0.7 copy.15
  4.4 0.7 concatenate.3.params.refs_0_
  5.1 1.4 compare_convert_fusion.1.refs_9_
  6.5 1.5 compare_convert_fusion.refs_8_
  8.0 1.7 constant_dynamic-slice_fusion.refs_3_
  9.7 2.2 fusion.refs_5_
  11.8 3.9 %reshape.50.aux.refs_12_ = f32[512,1024]{1,0:T(8,128)} reshape(f32[512,4,2,128]{3,2,1,0:T(2,128)} %param.11) | data formatting | bytes 4194304 | tf_op jit(solution)/shard_map/reshape | solution.py:467
  15.7 4.1 %shard_map.113 = (bf16[2,512,256]{2,1,0:T(8,128)(2,1)}, bf16[512,1024]{1,0:T(8,128)(2,1)}, bf16[512,512]{1,0:T(8,128)(2,1)}) custom-call(f32[4,7]{1,0:T(4,128)} %concatenate.3.params.refs_0_, f32[2,512,256]{2,1,0:T(8,128)} %refs_13_.1, f32[512,1024]{1,0:T(8,128)} %reshape.50.aux.refs_12_), custom_call_target="tpu_custom_call" | custom-call | tf_op jit(solution)/shard_map/pallas_call | solution.py:422
  19.8 19.9 %shard_map.114 = bf16[7,64,512]{2,1,0:T(8,128)(2,1)} custom-call(bf16[8,64,512]{2,1,0:T(8,128)(2,1)} %bitcast.26), custom_call_target="tpu_custom_call" | custom-call | tf_op jit(solution)/shard_map/pallas_call | solution.py:126
  39.7 1.1 convert_reduce_fusion.1
  40.8 1.5 fusion.2.refs_2_
  42.3 68.1 %shard_map.115 = (bf16[2,512,2048]{2,1,0:T(8,128)(2,1)}, bf16[2,2048,256]{2,1,0:T(8,128)(2,1)}, bf16[2048,1024]{1,0:T(8,128)(2,1)}, bf16[8,64,512]{2,1,0:T(8,128...) custom-call(bf16[2,512,256]{2,1,0:T(8,128)(2,1)} %get-tuple-element.23.refs_0_, ...), custom_call_target="tpu_custom_call" | custom-call | tf_op jit(solution)/shard_map/pallas_call | solution.py:276
  110.4 1.7 dynamic-slice_select_fusion.1
  112.1 14.1 %shard_map.116 = (f32[2,512,256]{2,1,0:T(8,128)}, f32[512,1024]{1,0:T(8,128)}, bf16[2,512,256]{2,1,0:T(8,128)(2,1)}, bf16[512,1024]{1,0:T(8,128)(2,1)}, bf16[512,512]{1,0:T(8,128)(2,1)}) custom-call(f32[4,7]{1,0:T(4,128)} %concatenate.3.params.refs_0_, bf16[512,2048]{1,0:T(8,128)(2,1)} %refs_1_.3, bf16[2048,1024]{1,0:T(8,128)(2,1)} %get-tuple-element.26.refs_2_, ...), custom_call_target="tpu_custom_call" | custom-call | tf_op jit(solution)/shard_map/pallas_call | solution.py:422
  126.1 16.3 %shard_map.117 = bf16[7,64,512]{2,1,0:T(8,128)(2,1)} custom-call(bf16[8,64,512]{2,1,0:T(8,128)(2,1)} %bitcast.24), custom_call_target="tpu_custom_call" | custom-call | tf_op jit(solution)/shard_map/pallas_call | solution.py:126
  142.4 1.1 convert_reduce_fusion
  143.5 1.5 fusion.1.refs_2_
  145.0 68.1 %shard_map.118 = (bf16[2,512,2048]{2,1,0:T(8,128)(2,1)}, bf16[2,2048,256]{2,1,0:T(8,128)(2,1)}, bf16[2048,1024]{1,0:T(8,128)(2,1)}, bf16[8,64,512]{2,1,0:T(8,128)(2,1)}, bf16[4,64,512]{2,1,0:T(8,128)(2,1)}) custom-call(bf16[2,512,256]{2,1,0:T(8,128)(2,1)} %get-tuple-element.32.refs_0_, bf16[2,256,1024]{2,1,0:T(8,128)(2,1)} %bitcast.22, ...), custom_call_target="tpu_custom_call" | custom-call | tf_op jit(solution)/shard_map/pallas_call | solution.py:276
  213.1 1.7 dynamic-slice_select_fusion
  214.8 13.7 %shard_map.119 = (f32[2,512,256]{2,1,0:T(8,128)}, f32[512,1024]{1,0:T(8,128)}) custom-call(f32[4,7]{1,0:T(4,128)} %concatenate.3.params.refs_0_, bf16[512,2048]{1,0:T(8,128)(2,1)} %refs_1_.3, bf16[2048,1024]{1,0:T(8,128)(2,1)} %get-tuple-element.35.refs_2_, bf16[2,512,2048]{2,1,0:T(8,128)(2,1)} %get-tuple-element.36.refs_3_, ...), custom_call_target="tpu_custom_call" | custom-call | tf_op jit(solution)/shard_map/pallas_call | solution.py:422
  228.5 4.0 %reshape.59 = f32[512,4,2,128]{3,2,1,0:T(2,128)} reshape(f32[512,1024]{1,0:T(8,128)} %get-tuple-element.43) | data formatting | bytes 4194304 | tf_op jit(solution)/shard_map/reshape | solution.py:535
  (2 shorter events, 0.0 us)

commit v3 on v2

--- a/solution.py
+++ b/solution.py
@@ -101,53 +101,19 @@
                 self.pair(*args).wait_send()
 
 
-def exchange_kernel(n_mode, src_ref, out_ref, send, recv):
-    me = lax.axis_index("mode")
-    copies = []
-    for d in range(1, n_mode):
-        target = lax.rem(me + d, n_mode)
-        origin = lax.rem(me + n_mode - d, n_mode)
-        out = pltpu.make_async_remote_copy(
-            src_ref=src_ref.at[target],
-            dst_ref=out_ref.at[d - 1],
-            send_sem=send.at[d - 1],
-            recv_sem=recv.at[d - 1],
-            device_id={"mode": target},
-            device_id_type=MESH,
-        )
-        out.start()
-        copies.append(out)
-    for out in copies:
-        out.wait()
-
-
-def exchange(partial):
-    n_mode = partial.shape[0]
-    return pl.pallas_call(
-        functools.partial(exchange_kernel, n_mode),
-        out_shape=jax.ShapeDtypeStruct((n_mode - 1,) + partial.shape[1:], partial.dtype),
-        in_specs=[ANY],
-        out_specs=ANY,
-        scratch_shapes=[
-            pltpu.SemaphoreType.DMA((n_mode - 1,)),
-            pltpu.SemaphoreType.DMA((n_mode - 1,)),
-        ],
-        compiler_params=pltpu.CompilerParams(has_side_effects=True),
-    )(partial)
-
-
 def gather_kernel(n_mode, n_row, wide, with_ham, *refs):
     n_in = 4 if with_ham else 3
-    rho, aux, chunk = refs[:3]
+    rho, aux, partial = refs[:3]
     ham = refs[3] if with_ham else None
     panel, cols, aux_all, sums, cross = refs[n_in : n_in + 5]
     ham_all = refs[n_in + 5] if with_ham else None
     rest = refs[n_in + 5 + (1 if with_ham else 0) :]
-    rho_stage, aux_stage, ham_stage, chunk_stage = rest[:4]
-    sems = rest[4:]
+    rho_stage, aux_stage, ham_stage, chunk_stage, parts = rest[:5]
+    sems = rest[5:]
     rows, columns = rho.shape[1], rho.shape[2]
     half = aux.shape[1]
-    chunk_rows = chunk.shape[0]
+    chunk_rows = partial.shape[1]
+    mode_me, row_me = lax.axis_index("mode"), lax.axis_index("row")
 
     def panel_at(slot, piece):
         if wide:
@@ -164,51 +130,83 @@
     def ham_at(slot, piece):
         return ham_all.at[pl.ds(pl.multiple_of(slot * rows, rows), rows), :]
 
+    def ham_own(piece):
+        if wide:
+            return ham.at[:, pl.ds(pl.multiple_of(mode_me * columns, columns), columns)]
+        return ham
+
     across = Gather("mode", n_mode, 2, lambda p: rho.at[p], panel_at, rho_stage.at[0], sems[0:3])
     down = Gather("row", n_row, 2, lambda p: rho.at[p], cols_at, rho_stage.at[1], sems[3:6])
     modes = Gather("row", n_row, 2, lambda p: aux.at[p], aux_at, aux_stage, sems[6:9])
     gathers = [across, down, modes]
     if with_ham:
-        gathers.insert(2, Gather("row", n_row, 1, lambda p: ham, ham_at, ham_stage, sems[9:12]))
-    chunk_send, chunk_recv, cross_send, cross_recv, chunk_local = sems[12:17]
-
-    mode_me, row_me = lax.axis_index("mode"), lax.axis_index("row")
+        gathers.insert(2, Gather("row", n_row, 1, ham_own, ham_at, ham_stage, sems[9:12]))
+    part_send, part_recv, chunk_send, chunk_recv, cross_send, cross_recv, chunk_local = sems[12:19]
     per = columns // chunk_rows
-    for g in gathers:
-        g.first()
-    for d in range(1, n_mode):
+
+    def part_copy(d):
         target = lax.rem(mode_me + d, n_mode)
-        pltpu.make_async_remote_copy(
-            src_ref=chunk,
-            dst_ref=sums.at[mode_me],
+        return pltpu.make_async_remote_copy(
+            src_ref=partial.at[target],
+            dst_ref=parts.at[d],
+            send_sem=part_send.at[d - 1],
+            recv_sem=part_recv.at[d - 1],
+            device_id={"mode": target},
+            device_id_type=MESH,
+        )
+
+    def chunk_copy(d, slot, target):
+        return pltpu.make_async_remote_copy(
+            src_ref=sums.at[mode_me],
+            dst_ref=sums.at[slot],
             send_sem=chunk_send.at[d - 1],
             recv_sem=chunk_recv.at[d - 1],
             device_id={"mode": target},
             device_id_type=MESH,
-        ).start()
-    wanted_by = (row_me * n_mode + mode_me) // per
-    for d in range(1, n_row):
-        pltpu.make_async_remote_copy(
-            src_ref=chunk,
-            dst_ref=cross.at[lax.rem(mode_me, per)],
+        )
+
+    def cross_copy(d, slot):
+        return pltpu.make_async_remote_copy(
+            src_ref=sums.at[mode_me],
+            dst_ref=cross.at[slot],
             send_sem=cross_send.at[d - 1],
-            recv_sem=cross_recv.at[lax.rem(mode_me, per)],
-            device_id={"mode": wanted_by, "row": lax.rem(row_me + d, n_row)},
+            recv_sem=cross_recv.at[slot],
+            device_id={
+                "mode": (row_me * n_mode + mode_me) // per,
+                "row": lax.rem(row_me + d, n_row),
+            },
             device_id_type=MESH,
-        ).start()
+        )
+
+    for g in gathers:
+        g.first()
+    for d in range(1, n_mode):
+        part_copy(d).start()
     for g in gathers:
         g.keep_load()
-    pltpu.make_async_copy(chunk, chunk_stage, chunk_local).start()
+    own_part = pltpu.make_async_copy(partial.at[mode_me], parts.at[0], chunk_local)
+    own_part.start()
     for g in gathers:
         g.keep_store()
-    pltpu.make_async_copy(chunk, chunk_stage, chunk_local).wait()
-    pltpu.make_async_copy(chunk_stage, sums.at[mode_me], chunk_local).start()
+    own_part.wait()
 
     across.step(0)
     for g in gathers[1:]:
         if g is not modes:
             for s in range(g.length - 1):
                 g.step(s)
+    total = parts[0].astype(jnp.float32)
+    for d in range(1, n_mode):
+        part_copy(d).wait_recv()
+        total = total + parts[d].astype(jnp.float32)
+    chunk_stage[...] = total.astype(chunk_stage.dtype)
+    kept = pltpu.make_async_copy(chunk_stage, sums.at[mode_me], chunk_local)
+    kept.start()
+    kept.wait()
+    for d in range(1, n_mode):
+        chunk_copy(d, mode_me, lax.rem(mode_me + d, n_mode)).start()
+    for d in range(1, n_row):
+        cross_copy(d, lax.rem(mode_me, per)).start()
     if n_mode // 2 > 2:
         across.step(1)
     for s in range(modes.length - 1):
@@ -219,41 +217,23 @@
     for g in gathers:
         g.keep_end()
         g.finish()
-    pltpu.make_async_copy(chunk_stage, sums.at[mode_me], chunk_local).wait()
     for d in range(1, n_mode):
+        part_copy(d).wait_send()
         origin = lax.rem(mode_me + n_mode - d, n_mode)
-        pltpu.make_async_remote_copy(
-            src_ref=chunk,
-            dst_ref=sums.at[origin],
-            send_sem=chunk_send.at[d - 1],
-            recv_sem=chunk_recv.at[d - 1],
-            device_id={"mode": origin},
-            device_id_type=MESH,
-        ).wait()
-    other_row = lax.rem(row_me + 1, n_row)
-
-    def cross_copy(slot, d):
-        return pltpu.make_async_remote_copy(
-            src_ref=chunk,
-            dst_ref=cross.at[slot],
-            send_sem=cross_send.at[d - 1],
-            recv_sem=cross_recv.at[slot],
-            device_id={"row": other_row},
-            device_id_type=MESH,
-        )
-
+        chunk_copy(d, origin, origin).wait()
     for d in range(1, n_row):
-        cross_copy(0, d).wait_send()
+        cross_copy(d, 0).wait_send()
 
     @pl.when((mode_me * columns) // rows != row_me)
     def _():
         for slot in range(per):
-            cross_copy(slot, 1).wait_recv()
-
-
-def gather(n_mode, n_row, rho, aux, chunk, ham):
+            cross_copy(1, slot).wait_recv()
+
+
+def gather(n_mode, n_row, rho, aux, partial, ham):
     _, rows, columns = rho.shape
     width = aux.shape[1]
+    chunk = jax.ShapeDtypeStruct(partial.shape[1:], partial.dtype)
     chunk_rows = chunk.shape[0]
     wide = columns % 128 == 0
     bf = jnp.bfloat16
@@ -283,6 +263,7 @@
             pltpu.VMEM(aux.shape, bf),
             pltpu.VMEM((1, rows, columns), bf),
             pltpu.VMEM(chunk.shape, bf),
+            pltpu.VMEM(partial.shape, bf),
         ]
         + group(n_mode, 2)
         + group(n_row, 2)
@@ -291,12 +272,14 @@
         + [
             dma((n_mode - 1,)),
             dma((n_mode - 1,)),
+            dma((n_mode - 1,)),
+            dma((n_mode - 1,)),
             dma((n_row - 1,)),
             dma((columns // chunk_rows,)),
             dma,
         ],
         compiler_params=pltpu.CompilerParams(has_side_effects=True),
-    )(*((rho, aux, chunk, ham) if with_ham else (rho, aux, chunk)))
+    )(*((rho, aux, partial, ham) if with_ham else (rho, aux, partial)))
 
 
 def lead_partial(params, aux, local_modes, lead_count, coupled):
@@ -325,14 +308,15 @@
 
 def stage_kernel(sizes, second, *refs):
     local_modes, lead_count, coupled = sizes
-    (params, ham, aux_all, panel, ham_all, all_select, cols) = refs[:7]
-    (gamma, row_select, col_select, sums, cross, aux) = refs[7:13]
+    params, places, ham, aux_all, panel, ham_all, cols, gamma, flat, sums, cross, aux = refs[:12]
+    all_select, col_select, cross_own = refs[-3:]
+    refs = refs[:-3]
     f32, bf = jnp.float32, jnp.bfloat16
     pairs = lead_count * coupled
     if second:
-        first_rho, first_aux, rho_out, aux_out = refs[13:]
+        first_rho, first_aux, rho_out, aux_out = refs[12:]
     else:
-        density, rho_out, aux_out, rho_b, aux_b, partial = refs[13:]
+        density, rho_out, aux_out, rho_b, aux_b, partial = refs[12:]
 
     def dot(x, y):
         return jnp.dot(x, y, preferred_element_type=f32)
@@ -340,6 +324,30 @@
     def dot_t(x, y):
         return lax.dot_general(x, y, (((1,), (1,)), ((), ())), preferred_element_type=f32)
 
+    block = aux.shape[0]
+    step = pl.program_id(0)
+    row_start, col_start, own_cross, cross_start = [places[i] for i in range(4)]
+
+    def select(start, count):
+        at = start + lax.broadcasted_iota(jnp.int32, (count, flat.shape[1]), 0)
+        return (at == flat[...]).astype(f32).astype(bf)
+
+    @pl.when(step == 0)
+    def _():
+        all_select[...] = select(0, all_select.shape[0])
+        col_select[...] = select(col_start, col_select.shape[0])
+
+        @pl.when(own_cross == 1)
+        def _():
+            columns = cross.shape[0]
+            cross_own[...] = sums[pl.ds(pl.multiple_of(cross_start, columns), columns), :]
+
+        @pl.when(own_cross == 0)
+        def _():
+            cross_own[...] = cross[...]
+
+    row_select = select(row_start + step * block, block)
+    own_sums = sums[pl.ds(pl.multiple_of(step * block, block), block), :]
     h = ham[...]
     rates = []
     source = []
@@ -347,8 +355,8 @@
         rho = panel[c]
         part = slice(c * pairs, (c + 1) * pairs)
         commutator = dot(h, cols[c]) - dot(rho, ham_all[...])
-        forward = dot_t(sums[:, part], col_select[...])
-        backward = dot_t(row_select[...], cross[:, part])
+        forward = dot_t(own_sums[:, part], col_select[...])
+        backward = dot_t(row_select, cross_own[:, part])
         rates.append((commutator, forward, backward))
         coupled_rho = dot(rho, all_select[...]).astype(bf)
         source.append(
@@ -413,7 +421,7 @@
     return pl.BlockSpec(sizes, lambda i: tuple(i if d == dim else 0 for d in range(len(shape))))
 
 
-def call(kernel, rows, inputs, outputs):
+def call(kernel, rows, inputs, outputs, scratch=()):
     block = 128 if rows % 128 == 0 else rows
     in_specs = [
         pl.BlockSpec(memory_space=pltpu.SMEM) if dim == "smem" else blocked(rows, block, x.shape, dim)
@@ -425,6 +433,7 @@
         out_shape=[jax.ShapeDtypeStruct(shape, dtype) for shape, dtype, _ in outputs],
         in_specs=in_specs,
         out_specs=[blocked(rows, block, shape, dim) for shape, _, dim in outputs],
+        scratch_shapes=list(scratch),
         compiler_params=pltpu.CompilerParams(
             dimension_semantics=("arbitrary",), vmem_limit_bytes=56 * 2**20
         ),
@@ -456,10 +465,9 @@
     chunk_rows = rows // n_mode
     flat = coupling.reshape(-1)
     pairs = lead_count * coupled
-    own_columns = lax.dynamic_slice_in_dim(hamiltonian, col_start, columns, 1)
-    row_select = (row_start + jnp.arange(rows, dtype=jnp.int32)[:, None] == flat[None, :]).astype(bf)
-    col_select = (col_start + jnp.arange(columns, dtype=jnp.int32)[:, None] == flat[None, :]).astype(bf)
-    all_select = (jnp.arange(n_mode * columns, dtype=jnp.int32)[:, None] == flat[None, :]).astype(bf)
+    own_columns = hamiltonian
+    if columns % 128:
+        own_columns = lax.dynamic_slice_in_dim(hamiltonian, col_start, columns, 1)
     onehot = (lead_index[:, None] == jnp.arange(lead_count, dtype=jnp.int32)[None, :]).astype(f32)
     params = jnp.concatenate(
         [mode_level[:, None], mode_width[:, None], residue, occupation[:, None], onehot], axis=1
@@ -468,40 +476,48 @@
     width = aux.shape[1]
     sizes = (local_modes, lead_count, coupled)
     cross_row = col_start // rows
-    cross_chunk = lax.rem(mode_me, rows // columns) * (columns // chunk_rows)
+    places = jnp.stack(
+        [
+            row_start,
+            col_start,
+            (cross_row == row_me).astype(jnp.int32),
+            lax.rem(mode_me, rows // columns) * columns,
+        ]
+    )
 
     rho_shape, aux_shape, sum_shape = density.shape, aux.shape, (rows, 2 * pairs)
 
     def moved(rho_b, aux_b, partial, ham):
         partial = partial.reshape(n_mode, chunk_rows, 2 * pairs)
-        own = lax.dynamic_index_in_dim(partial, mode_me, 0, keepdims=False)
-        others = exchange(partial)
-        chunk = (own.astype(f32) + jnp.sum(others.astype(f32), axis=0)).astype(bf)
-        out = gather(n_mode, n_row, rho_b, aux_b, chunk, ham)
+        out = gather(n_mode, n_row, rho_b, aux_b, partial, ham)
         panel, cols, aux_all, sums, cross = out[:5]
         if panel.ndim == 4:
             panel = panel.transpose(1, 2, 0, 3).reshape(2, rows, -1)
-        own = lax.dynamic_slice_in_dim(sums, cross_chunk, columns // chunk_rows, 0)
-        cross = jnp.where(cross_row == row_me, own, cross).reshape(columns, 2 * pairs)
+        cross = cross.reshape(columns, 2 * pairs)
         return panel, cols, aux_all, sums.reshape(rows, 2 * pairs), cross, out[5:]
 
     def stage(second, ham_all, panel, cols, aux_all, sums, cross, extra, outputs):
         inputs = [
             (params, "smem"),
+            (places, "smem"),
             (hamiltonian, 0),
             (aux_all, None),
             (panel, 1),
             (ham_all, None),
-            (all_select, None),
             (cols, None),
             (lead_gamma, None),
-            (row_select, 0),
-            (col_select, None),
-            (sums, 0),
+            (flat[None, :], None),
+            (sums, None),
             (cross, None),
             (aux, 0),
         ] + extra
-        return call(functools.partial(stage_kernel, sizes, second), rows, inputs, outputs)
+        scratch = [
+            pltpu.VMEM((n_mode * columns, pairs), bf),
+            pltpu.VMEM((columns, pairs), bf),
+            pltpu.VMEM((columns, 2 * pairs), bf),
+        ]
+        kernel = functools.partial(stage_kernel, sizes, second)
+        return call(kernel, rows, inputs, outputs, scratch)
 
     rho_b, aux_b, partial = call(
         functools.partial(prepare_kernel, sizes),

time: 233 us -> 195 us (0.84)
  Pallas kernels: 204 us -> 181 us
  other arithmetic: 14.4 us -> 1.38 us
    pallas_call x2 -> x0, Pallas kernels: 36.1 us -> none  [exchange(): pl.pallas_call(functools.partial(exchange_kernel, n_mode), out_shape=jax....]
    pallas_call x2, Pallas kernels: 136 us -> 149 us  [gather(): pl.pallas_call(functools.partial(gather_kernel, n_mode, n_row, wide, with...]
    convert_element_type x5 -> x0, other arithmetic: 8.06 us -> none  [the longest x2 2.96 us: moved(): chunk = (own.astype(f32) + jnp.sum(others.astype(f32), axis=0)).astype(bf)]
    select_n x2 -> x0, other arithmetic: 3.41 us -> none  [moved(): jnp.where(cross_row == row_me, own, cross).reshape(columns, 2 * pairs)]
where the time goes in v3:
time: 195 us
  Pallas kernels  181 us (93%)
  local copies, waits for them, and re-layouts  11.5 us (6%)
    pallas_call x2, Pallas kernels, gather(): pl.pallas_call(functools.partial(gather_kernel, n_mode, n_row, wide, with...  149 us
    pallas_call x3, Pallas kernels, call(): pl.pallas_call(kernel, grid=(rows // block,), out_shape=[jax.ShapeDtypeSt...  32 us
    reshape x1, local copies, waits for them, and re-layouts, shards(): return (rho_out, aux_out.reshape(auxiliary.shape))  3.98 us

profile of v3, /device:TPU:0, one launch (start us, length us, event | category | flops | bytes accessed | tf_op | source)
XLA Modules:
  0.0 194.6 jit_solution(12120382483314751447)
XLA Ops:
  0.6 0.7 pad_add_fusion.refs_1_
  1.3 0.7 fusion
  2.0 0.7 copy.12
  2.8 0.7 copy.13
  3.5 0.8 copy.14
  4.3 0.7 copy.15
  5.0 0.7 concatenate.3.params.refs_0_
  5.7 3.9 %reshape.35.aux.refs_11_ = f32[512,1024]{1,0:T(8,128)} reshape(f32[512,4,2,128]{3,2,1,0:T(2,128)} %param.11) | data formatting | bytes 4194304 | tf_op jit(solution)/shard_map/reshape | solution.py:475
  9.6 4.1 %shard_map.113 = (bf16[2,512,256]{2,1,0:T(8,128)(2,1)}, bf16[512,1024]{1,0:T(8,128)(2,1)}, bf16[512,512]{1,0:T(8,128)(2,1)}) custom-call(f32[4,7]{1,0:T(4,128)} %concatenate.3.params.refs_0_, f32[2,512,256]{2,1,0:T(8,128)} %refs_12_.1, f32[512,1024]{1,0:T(8,128)} %reshape.35.aux.refs_11_), custom_call_target="tpu_custom_call" | custom-call | tf_op jit(solution)/shard_map/pallas_call | solution.py:430
  13.7 75.5 %shard_map.114 = (bf16[2,512,2048]{2,1,0:T(8,128)(2,1)}, bf16[2,2048,256]{2,1,0:T(8,128)(2,1)}, bf16[2048,1024]{1,0:T(8,128)(2,1)}, bf16[8,64,512]{2,1,0:T(8,128...) custom-call(bf16[2,512,256]{2,1,0:T(8,128)(2,1)} %get-tuple-element.23.refs_0_, ...), custom_call_target="tpu_custom_call" | custom-call | tf_op jit(solution)/shard_map/pallas_call | solution.py:256
  89.2 14.1 %shard_map.115 = (f32[2,512,256]{2,1,0:T(8,128)}, f32[512,1024]{1,0:T(8,128)}, bf16[2,512,256]{2,1,0:T(8,128)(2,1)}, bf16[512,1024]{1,0:T(8,128)(2,1)}, bf16[512,512]{1,0:T(8,128)(2,1)}) custom-call(f32[4,7]{1,0:T(4,128)} %concatenate.3.params.refs_0_, s32[4]{0:T(128)} %pad_add_fusion.refs_1_, bf16[512,2048]{1,0:T(8,128)(2,1)} %refs_2_.3, ...), custom_call_target="tpu_custom_call" | custom-call | tf_op jit(solution)/shard_map/pallas_call | solution.py:430
  103.3 73.5 %shard_map.116 = (bf16[2,512,2048]{2,1,0:T(8,128)(2,1)}, bf16[2,2048,256]{2,1,0:T(8,128)(2,1)}, bf16[2048,1024]{1,0:T(8,128)(2,1)}, bf16[8,64,512]{2,1,0:T(8,128)(2,1)}, bf16[4,64,512]{2,1,0:T(8,128)(2,1)}) custom-call(bf16[2,512,256]{2,1,0:T(8,128)(2,1)} %get-tuple-element.32.refs_0_, bf16[2,256,1024]{2,1,0:T(8,128)(2,1)} %bitcast.16, ...), custom_call_target="tpu_custom_call" | custom-call | tf_op jit(solution)/shard_map/pallas_call | solution.py:256
  176.8 13.8 %shard_map.117 = (f32[2,512,256]{2,1,0:T(8,128)}, f32[512,1024]{1,0:T(8,128)}) custom-call(f32[4,7]{1,0:T(4,128)} %concatenate.3.params.refs_0_, s32[4]{0:T(128)} %pad_add_fusion.refs_1_, bf16[512,2048]{1,0:T(8,128)(2,1)} %refs_2_.3, bf16[2048,1024]{1,0:T(8,128)(2,1)} %get-tuple-element.35.refs_3_, bf16[2,512,2048]{2,1,0:T(8,128)(2,1)} %get-tuple-element.36.refs_4_, ...), custom_call_target="tpu_custom_call" | custom-call | tf_op jit(solution)/shard_map/pallas_call | solution.py:430
  190.6 4.0 %reshape.44 = f32[512,4,2,128]{3,2,1,0:T(2,128)} reshape(f32[512,1024]{1,0:T(8,128)} %get-tuple-element.43) | data formatting | bytes 4194304 | tf_op jit(solution)/shard_map/reshape | solution.py:551

commit v4 on v3

--- a/solution.py
+++ b/solution.py
@@ -108,8 +108,8 @@
     panel, cols, aux_all, sums, cross = refs[n_in : n_in + 5]
     ham_all = refs[n_in + 5] if with_ham else None
     rest = refs[n_in + 5 + (1 if with_ham else 0) :]
-    rho_stage, aux_stage, ham_stage, chunk_stage, parts = rest[:5]
-    sems = rest[5:]
+    rho_stage, aux_stage, ham_stage, chunk_stage, parts, part_stage = rest[:6]
+    sems = rest[6:]
     rows, columns = rho.shape[1], rho.shape[2]
     half = aux.shape[1]
     chunk_rows = partial.shape[1]
@@ -118,8 +118,8 @@
     def panel_at(slot, piece):
         if wide:
             start = pl.multiple_of(slot * columns, columns)
-            return panel.at[piece, :, pl.ds(start, columns)]
-        return panel.at[slot, piece]
+            return panel.at[piece // 2, pl.ds(piece % 2 * half, half), pl.ds(start, columns)]
+        return panel.at[slot, piece // 2, pl.ds(piece % 2 * half, half)]
 
     def cols_at(slot, piece):
         return cols.at[piece, pl.ds(pl.multiple_of(slot * rows, rows), rows), :]
@@ -129,14 +129,17 @@
 
     def ham_at(slot, piece):
         return ham_all.at[pl.ds(pl.multiple_of(slot * rows, rows), rows), :]
+
+    def rho_at(piece):
+        return rho.at[piece // 2, pl.ds(piece % 2 * half, half), :]
 
     def ham_own(piece):
         if wide:
             return ham.at[:, pl.ds(pl.multiple_of(mode_me * columns, columns), columns)]
         return ham
 
-    across = Gather("mode", n_mode, 2, lambda p: rho.at[p], panel_at, rho_stage.at[0], sems[0:3])
-    down = Gather("row", n_row, 2, lambda p: rho.at[p], cols_at, rho_stage.at[1], sems[3:6])
+    across = Gather("mode", n_mode, 4, rho_at, panel_at, part_stage, sems[0:3])
+    down = Gather("row", n_row, 2, lambda p: rho.at[p], cols_at, rho_stage, sems[3:6])
     modes = Gather("row", n_row, 2, lambda p: aux.at[p], aux_at, aux_stage, sems[6:9])
     gathers = [across, down, modes]
     if with_ham:
@@ -259,13 +262,14 @@
         in_specs=[ANY] * (4 if with_ham else 3),
         out_specs=[ANY] * len(shapes),
         scratch_shapes=[
-            pltpu.VMEM((2, 2, rows, columns), bf),
+            pltpu.VMEM((2, rows, columns), bf),
             pltpu.VMEM(aux.shape, bf),
             pltpu.VMEM((1, rows, columns), bf),
             pltpu.VMEM(chunk.shape, bf),
             pltpu.VMEM(partial.shape, bf),
+            pltpu.VMEM((4, rows // 2, columns), bf),
         ]
-        + group(n_mode, 2)
+        + group(n_mode, 4)
         + group(n_row, 2)
         + group(n_row, 2)
         + group(n_row, 1)

time: 195 us -> 192 us (0.985)
  Pallas kernels: 181 us -> 178 us
    pallas_call x2, Pallas kernels: 149 us -> 146 us  [gather(): pl.pallas_call(functools.partial(gather_kernel, n_mode, n_row, wide, with...]
where the time goes in v4:
time: 192 us; the launch traced here: 191 us
  Pallas kernels  178 us (93%)
  local copies, waits for them, and re-layouts  11.5 us (6%)
    pallas_call x2, Pallas kernels, gather(): pl.pallas_call(functools.partial(gather_kernel, n_mode, n_row, wide, with...  146 us
    pallas_call x3, Pallas kernels, call(): pl.pallas_call(kernel, grid=(rows // block,), out_shape=[jax.ShapeDtypeSt...  32 us
    reshape x1, local copies, waits for them, and re-layouts, shards(): return (rho_out, aux_out.reshape(auxiliary.shape))  3.98 us
    reshape x1, local copies, waits for them, and re-layouts, shards(): aux = auxiliary.reshape(rows, -1)  3.88 us

profile of v4, /device:TPU:0, one launch (start us, length us, event | category | flops | bytes accessed | tf_op | source)
XLA Modules:
  0.0 191.1 jit_solution(9959030084671264763)
XLA Ops:
  0.6 0.7 pad_add_fusion.refs_1_
  1.3 0.7 fusion
  2.0 0.7 copy.12
  2.8 0.7 copy.13
  3.5 0.8 copy.14
  4.3 0.7 copy.15
  5.0 0.7 concatenate.3.params.refs_0_
  5.7 3.9 %reshape.35.aux.refs_11_ = f32[512,1024]{1,0:T(8,128)} reshape(f32[512,4,2,128]{3,2,1,0:T(2,128)} %param.11) | data formatting | bytes 4194304 | tf_op jit(solution)/shard_map/reshape | solution.py:479
  9.6 4.1 %shard_map.113 = (bf16[2,512,256]{2,1,0:T(8,128)(2,1)}, bf16[512,1024]{1,0:T(8,128)(2,1)}, bf16[512,512]{1,0:T(8,128)(2,1)}) custom-call(f32[4,7]{1,0:T(4,128)} %concatenate.3.params.refs_0_, f32[2,512,256]{2,1,0:T(8,128)} %refs_12_.1, f32[512,1024]{1,0:T(8,128)} %reshape.35.aux.refs_11_), custom_call_target="tpu_custom_call" | custom-call | tf_op jit(solution)/shard_map/pallas_call | solution.py:434
  13.7 74.6 %shard_map.114 = (bf16[2,512,2048]{2,1,0:T(8,128)(2,1)}, bf16[2,2048,256]{2,1,0:T(8,128)(2,1)}, bf16[2048,1024]{1,0:T(8,128)(2,1)}, bf16[8,64,512]{2,1,0:T(8,128...) custom-call(bf16[2,512,256]{2,1,0:T(8,128)(2,1)} %get-tuple-element.23.refs_0_, ...), custom_call_target="tpu_custom_call" | custom-call | tf_op jit(solution)/shard_map/pallas_call | solution.py:259
  88.2 14.1 %shard_map.115 = (f32[2,512,256]{2,1,0:T(8,128)}, f32[512,1024]{1,0:T(8,128)}, bf16[2,512,256]{2,1,0:T(8,128)(2,1)}, bf16[512,1024]{1,0:T(8,128)(2,1)}, bf16[512,512]{1,0:T(8,128)(2,1)}) custom-call(f32[4,7]{1,0:T(4,128)} %concatenate.3.params.refs_0_, s32[4]{0:T(128)} %pad_add_fusion.refs_1_, bf16[512,2048]{1,0:T(8,128)(2,1)} %refs_2_.3, ...), custom_call_target="tpu_custom_call" | custom-call | tf_op jit(solution)/shard_map/pallas_call | solution.py:434
  102.3 71.0 %shard_map.116 = (bf16[2,512,2048]{2,1,0:T(8,128)(2,1)}, bf16[2,2048,256]{2,1,0:T(8,128)(2,1)}, bf16[2048,1024]{1,0:T(8,128)(2,1)}, bf16[8,64,512]{2,1,0:T(8,128)(2,1)}, bf16[4,64,512]{2,1,0:T(8,128)(2,1)}) custom-call(bf16[2,512,256]{2,1,0:T(8,128)(2,1)} %get-tuple-element.32.refs_0_, bf16[2,256,1024]{2,1,0:T(8,128)(2,1)} %bitcast.16, ...), custom_call_target="tpu_custom_call" | custom-call | tf_op jit(solution)/shard_map/pallas_call | solution.py:259
  173.3 13.8 %shard_map.117 = (f32[2,512,256]{2,1,0:T(8,128)}, f32[512,1024]{1,0:T(8,128)}) custom-call(f32[4,7]{1,0:T(4,128)} %concatenate.3.params.refs_0_, s32[4]{0:T(128)} %pad_add_fusion.refs_1_, bf16[512,2048]{1,0:T(8,128)(2,1)} %refs_2_.3, bf16[2048,1024]{1,0:T(8,128)(2,1)} %get-tuple-element.35.refs_3_, bf16[2,512,2048]{2,1,0:T(8,128)(2,1)} %get-tuple-element.36.refs_4_, ...), custom_call_target="tpu_custom_call" | custom-call | tf_op jit(solution)/shard_map/pallas_call | solution.py:434
  187.2 4.0 %reshape.44 = f32[512,4,2,128]{3,2,1,0:T(2,128)} reshape(f32[512,1024]{1,0:T(8,128)} %get-tuple-element.43) | data formatting | bytes 4194304 | tf_op jit(solution)/shard_map/reshape | solution.py:555
